TPU v7x, 8 devices: a whole 2x2x1 slice. The times are simulated.
8 devices in a mesh: dp: 2 (over z, y), tp: 4 (over x, core).
Axes of the slice: x: 2, y: 2, z: 1, core: 2. Of those that a mesh axis runs over, the one named last changes fastest.
Arguments:
- hidden: bfloat16 [128, 5120], P('dp'), parts along dimension 0
- cache_len: int32 [128], P('dp'), parts along dimension 0
- lin_state: float32 [128, 32, 128, 128], P('dp', 'tp'), parts along dimension 0
- k_cache: bfloat16 [128, 8, 512, 128], P('dp', 'tp'), parts along dimension 0
- v_cache: bfloat16 [128, 8, 512, 128], P('dp', 'tp'), parts along dimension 0
- norm_first: float32 [5120], replicated
- w_qkv: bfloat16 [5120, 3, 32, 128], P(None, None, 'tp')
- w_gate: bfloat16 [5120, 32, 128], P(None, 'tp')
- slopes: float32 [32], P('tp')
- out_norm: float32 [32, 128], P('tp')
- w_out_lin: bfloat16 [32, 128, 5120], P('tp')
- norm_second: float32 [5120], replicated
- w_attn: bfloat16 [5120, 8, 6, 128], P(None, 'tp')
- w_out_attn: bfloat16 [32, 128, 5120], P('tp')
- mix_alpha: float32 [2], replicated
- mix_beta: float32 [2], replicated
Outputs:
- output 1: bfloat16 [128, 5120], P('dp'), parts along dimension 0
- output 2: float32 [128, 32, 128, 128], P('dp', 'tp'), parts along dimension 0
- output 3: bfloat16 [128, 8, 512, 128], P('dp', 'tp'), parts along dimension 0
- output 4: bfloat16 [128, 8, 512, 128], P('dp', 'tp'), parts along dimension 0
There are 2 independent parts. A program takes and returns all parts, laid end to end along the dimension named above; an argument that names none is the same for every part.
All inputs are finite; a program needn't handle non-finite values.
Results may differ from a plain program's by a relative error of at most 0.0113869.
Values sent between devices are 32-bit elements.
A program may use at most 1 GiB of HBM per device.

v0:
```python
import jax
import jax.numpy as jnp
from jax import lax
from jax.sharding import PartitionSpec as P

EPS = 1e-5
ROPE_BASE = 10000000.0


def rms_scale(values, gain_vec):
    wide_vals = values.astype(jnp.float32)
    return wide_vals * lax.rsqrt(jnp.mean(wide_vals * wide_vals, axis=-1, keepdims=True) + EPS) * gain_vec


def rotary(values, positions):
    rot_dim = values.shape[-1] // 2
    half_dim = rot_dim // 2
    inv_freq = ROPE_BASE ** (-2.0 * jnp.arange(half_dim, dtype=jnp.float32) / rot_dim)
    angles = positions.astype(jnp.float32)[:, None] * inv_freq[None, :]
    cosine = jnp.cos(angles)[:, None, None, :]
    sine_val = jnp.sin(angles)[:, None, None, :]
    rot_first = values[..., :half_dim]
    rot_second = values[..., half_dim:rot_dim]
    return jnp.concatenate([rot_first * cosine - rot_second * sine_val,
                            rot_second * cosine + rot_first * sine_val,
                            values[..., rot_dim:]], axis=-1)


def solution(mesh):
    tp_size = mesh.shape['tp']
    row_spec = P('dp', None)
    cache_spec = P('dp', 'tp', None, None)
    in_specs = (row_spec, P('dp'), cache_spec, cache_spec, cache_spec, P(None), P(None, None, 'tp', None),
                P(None, 'tp', None), P('tp'), P('tp', None), P('tp', None, None), P(None),
                P(None, 'tp', None, None), P('tp', None, None), P(None), P(None))
    out_specs = (row_spec, cache_spec, cache_spec, cache_spec)

    def local_step(hidden, cache_len, lin_state, k_cache, v_cache, norm_first, w_qkv, w_gate, slopes, out_norm,
                   w_out_lin, norm_second, w_attn, w_out_attn, mix_alpha, mix_beta):
        head_dim = k_cache.shape[3]
        full_width = w_out_lin.shape[0] * head_dim * tp_size
        kv_local = w_attn.shape[1]
        group_size = w_attn.shape[2] - 2
        h_first = rms_scale(hidden, norm_first).astype(jnp.bfloat16)
        proj_lin = jax.nn.silu(jnp.einsum('bd,dchk->bchk', h_first, w_qkv, preferred_element_type=jnp.float32)).astype(jnp.bfloat16)
        decay_rate = jnp.exp(-slopes)[None, :, None, None]
        state_out = decay_rate * lin_state + jnp.einsum('bhk,bhv->bhkv', proj_lin[:, 1], proj_lin[:, 2], preferred_element_type=jnp.float32)
        lin_attn = jnp.einsum('bhk,bhkv->bhv', proj_lin[:, 0].astype(jnp.float32), state_out, precision=lax.Precision.HIGHEST)
        sq_sum = lax.psum(jnp.sum(lin_attn * lin_attn, axis=(1, 2)), 'tp')
        inv_rms = lax.rsqrt(sq_sum / full_width + EPS)[:, None, None]
        gate_val = jax.nn.sigmoid(jnp.einsum('bd,dhk->bhk', h_first, w_gate, preferred_element_type=jnp.float32))
        gated_out = (lin_attn * inv_rms * out_norm * gate_val).astype(jnp.bfloat16)
        lin_part = jnp.einsum('bhk,hkd->bd', gated_out, w_out_lin, preferred_element_type=jnp.float32)
        lin_out = lax.psum(lin_part, 'tp')
        mid_hidden = (mix_alpha[0] * h_first.astype(jnp.float32) + mix_beta[0] * lin_out).astype(jnp.bfloat16)
        h_second = rms_scale(mid_hidden, norm_second).astype(jnp.bfloat16)
        proj_attn = jnp.einsum('bd,dkjc->bkjc', h_second, w_attn, preferred_element_type=jnp.float32)
        turned = rotary(proj_attn[:, :, :group_size + 1], cache_len).astype(jnp.bfloat16)
        key_new = turned[:, :, group_size][:, :, None, :]
        value_new = proj_attn[:, :, group_size + 1].astype(jnp.bfloat16)[:, :, None, :]
        positions = jnp.arange(k_cache.shape[2], dtype=jnp.int32)
        write_mask = (positions[None, :] == cache_len[:, None])[:, None, :, None]
        k_out = jnp.where(write_mask, key_new, k_cache)
        v_out = jnp.where(write_mask, value_new, v_cache)
        scores = jnp.einsum('bkgc,bktc->bkgt', turned[:, :, :group_size], k_out, preferred_element_type=jnp.float32) * head_dim ** -0.5
        valid_mask = (positions[None, :] <= cache_len[:, None])[:, None, None, :]
        probs_bf = jax.nn.softmax(jnp.where(valid_mask, scores, -jnp.inf), axis=-1).astype(jnp.bfloat16)
        attn_rows = jnp.einsum('bkgt,bktc->bkgc', probs_bf, v_out, preferred_element_type=jnp.float32).astype(jnp.bfloat16)
        w_out_grouped = w_out_attn.reshape(kv_local, group_size, head_dim, w_out_attn.shape[2])
        attn_part = jnp.einsum('bkgc,kgcd->bd', attn_rows, w_out_grouped, preferred_element_type=jnp.float32)
        attn_out = lax.psum(attn_part, 'tp')
        hidden_out = (mix_alpha[1] * h_second.astype(jnp.float32) + mix_beta[1] * attn_out).astype(jnp.bfloat16)
        return hidden_out, state_out, k_out, v_out

    return jax.shard_map(local_step, mesh=mesh, in_specs=in_specs, out_specs=out_specs, check_vma=False)
```

profile of v0, /device:TPU:0, one launch (start us, length us, event | category | flops | bytes accessed | tf_op | source)
XLA Modules:
  0.0 228.8 jit_solution(3295842133227921452)
XLA Ops:
  7.2 0.0 all-reduce.3.cloned.1.call-start
  7.2 0.7 negate_exponential_fusion
  7.9 1.3 fusion.15
  9.2 15.7 %multiply_convert_fusion = bf16[64,3,8,128]{3,0,2,1:T(8,128)(2,1)S(1)} fusion(bf16[5120,3,8,128]{3,2,1,0:T(8,128)(2,1)} %param.22, bf16[64,5120]{1,0:T(8,128)(2,1)} %param.16, f32[5120]{0:T(1024)} %param.21, f32[64]{0:T(128)S(1)} %add_rsqrt_fusion.2), kind=kOutput, calls=%fused_computation.37 | convolution fusion | flops 2015559680 | bytes 32526592 | tf_op jit(solution)/shard_map/bd,dchk->bchk/dot_general | solution.py:45
  25.0 0.2 copy.22
  25.1 0.2 copy.21
  25.3 22.7 %multiply_add_fusion = f32[64,8,128,128]{3,2,1,0:T(8,128)} fusion(f32[64,8,128,128]{3,2,1,0:T(8,128)} %param.18, f32[64,8,128]{2,1,0:T(8,128)S(1)} %copy.22, f32[64,8,128]{2,1,0:T(8,128)S(1)} %copy.21, f32[8]{0:T(128)S(1)} %negate_exponential_fusion), kind=kLoop, calls=%fused_computation.1 | loop fusion | flops 25165824 | bytes 67633184 | tf_op jit(solution)/shard_map/add | solution.py:47
  48.1 19.1 %fusion.48 = f32[64,8,1,128]{3,2,1,0:T(1,128)S(1)} fusion(f32[64,8,128,128]{3,2,1,0:T(8,128)} %multiply_add_fusion, bf16[64,8,128,1]{2,0,1,3:T(8,128)(2,1)S(1)} %get-tuple-element.8), kind=kOutput, calls=%fused_computation.50 | convolution fusion | flops 100663296 | bytes 33947648 | tf_op jit(solution)/shard_map/bhk,bhkv->bhv/dot_general | solution.py:48
  67.2 0.1 fusion.46
  67.3 8.9 %psum.21 = f32[64]{0:T(128)S(1)} all-reduce(f32[64]{0:T(128)S(1)} %fusion.46), channel_id=1, replica_groups=mesh['dp'=2,'tp'=4] {'tp'}, use_global_device_ids=true, to_apply=%region_2.3 | all-reduce | flops 64 | bytes 512 | tf_op jit(solution)/shard_map/psum | solution.py:49
  76.3 6.0 %fusion.36 = bf16[64,8,128]{2,0,1:T(8,128)(2,1)S(1)} fusion(bf16[5120,8,128]{2,1,0:T(8,128)(2,1)} %param.23, f32[64,8,1,128]{3,2,1,0:T(1,128)S(1)} %fusion.48, f32[8,128]{1,0:T(8,128)S(1)} %copy-done.6, f32[64]{0:T(128)S(1)} %add_rsqrt_fusion.1, bf16[64,5120]{1,0:T(8,128)(2,1)S(1)} %copy-done, f32[5120]{0:T(1024)S(1)} %copy-done.1, f32[64]{0:T(128)S(1)} %add_rsqrt_fusion.2), kind=kOutput, calls=%fused_computation.35 | convolution fusion | flops 672858112 | bytes 11559424 | tf_op jit(solution)/shard_map/bd,dhk->bhk/dot_general | solution.py:51
  82.3 7.0 %convolution_bitcast_fusion = f32[64,5120]{1,0:T(8,128)} fusion(bf16[64,8,128]{2,0,1:T(8,128)(2,1)S(1)} %fusion.36, bf16[8,128,5120]{2,1,0:T(8,128)(2,1)} %param.26), kind=kOutput, calls=%fused_computation.12 | convolution fusion | flops 671088640 | bytes 11927552 | tf_op jit(solution)/shard_map/bhk,hkd->bd/dot_general | solution.py:53
  89.4 0.0 all-reduce.3.cloned.1.call-update
  89.4 0.0 all-reduce.5.cloned.1.call-start
  89.5 0.7 fusion.56
  90.1 0.6 fusion.57
  90.7 0.1 iota_compare_fusion.1
  90.9 0.2 multiply_cosine_fusion
  91.1 32.3 %all-reduce.3.cloned.1.call-done = f32[64,5120]{1,0:T(8,128)} async-done(((f32[64,5120]{1,0:T(8,128)}), f32[64,5120]{1,0:T(8,128)}) %all-reduce.3.cloned.1.call-update) | async-done | bytes 1310736 | tf_op jit(solution)/shard_map/psum | solution.py:54
  123.3 3.1 %fusion.18 = (f32[64]{0:T(128)S(1)}, bf16[64,5120]{1,0:T(8,128)(2,1)S(1)}) fusion(f32[64,5120]{1,0:T(8,128)} %all-reduce.3.cloned.1.call-done, f32[]{:T(128)} %bitcast.2, f32[5120]{0:T(1024)S(1)} %copy-done.1, f32[64]{0:T(128)S(1)} %add_rsqrt_fusion.2, bf16[64,5120]{1,0:T(8,128)(2,1)S(1)} %copy-done, f32[]{:T(128)} %bitcast.1), kind=kLoop, calls=%fused_computation.25 | loop fusion | flops 3932096 | bytes 2642440 | tf_op jit(solution)/shard_map/reduce_sum | solution.py:12
  126.5 9.6 %fusion.58 = (bf16[64,2,6,128]{3,0,2,1:T(8,128)(2,1)S(1)}, f32[64,2,6,128]{3,0,2,1:T(8,128)S(1)}) fusion(bf16[5120,2,6,128]{3,1,2,0:T(2,128)(2,1)} %param.28, f32[5120]{0:T(1024)S(1)} %copy-done.2, f32[64]{0:T(128)S(1)} %add_rsqrt_fusion, bf16[64,5120]{1,0:T(8,128)(2,1)S(1)} %get-tuple-element.5), kind=kOutput, calls=%fused_computation.72 | convolution fusion | flops 1008041984 | bytes 16994560 | tf_op jit(solution)/shard_map/bd,dkjc->bkjc/dot_general | solution.py:57
  136.1 0.1 slice.63
  136.2 0.2 subtract_convert_fusion
  136.4 0.1 maximum_bitcast_fusion
  136.5 0.2 pad_maximum_fusion
  136.8 23.1 %broadcast_select_fusion.1 = (bf16[64,2,512,128]{3,2,1,0:T(8,128)(2,1)}, bf16[64,2,512,128]{3,2,1,0:T(8,128)(2,1)}) fusion(bf16[64,2,512,128]{3,2,1,0:T(8,128)(2,1)} %param.19, pred[64,512]{1,0:T(8,128)(4,1)S(1)} %get-tuple-element.20, bf16[64,2,128]{2,1,0:T(2,128)(2,1)S(1)} %copy.24, bf16[64,2,512,128]{3,2,1,0:T(8,128)(2,1)} %param.20, ...), kind=kLoop, calls=%fused_computation.5 | loop fusion | flops 16777216 | bytes 67207168 | tf_op jit(solution)/shard_map/jit(_where)/select_n | solution.py:63
  159.9 10.4 %fusion.59 = (f32[64,2,4]{2,1,0:T(2,128)S(1)}, f32[64,2,4,512]{3,2,1,0:T(4,128)S(1)}) fusion(bf16[64,2,512,128]{3,2,1,0:T(8,128)(2,1)} %get-tuple-element.11, pred[64,512]{1,0:T(8,128)(4,1)S(1)} %get-tuple-element.19, bf16[64,2,4,128]{3,0,2,1:T(8,128)(2,1)S(1)} %slice.64), kind=kOutput, calls=%fused_computation.73 | convolution fusion | flops 68157952 | bytes 17991680 | tf_op jit(solution)/shard_map/sub | solution.py:67
  170.3 7.1 %fusion.44 = bf16[64,2,4,128]{3,2,1,0:T(4,128)(2,1)S(1)} fusion(bf16[64,2,512,128]{3,2,1,0:T(8,128)(2,1)} %get-tuple-element.12, f32[64,2,4,512]{3,2,1,0:T(4,128)S(1)} %get-tuple-element.24, f32[64,2,4]{2,1,0:T(2,128)S(1)} %get-tuple-element.23), kind=kOutput, calls=%fused_computation.41 | convolution fusion | flops 67633152 | bytes 17958912 | tf_op jit(solution)/shard_map/bkgt,bktc->bkgc/dot_general | solution.py:68
  177.4 7.0 %fusion.9 = f32[64,5120]{1,0:T(8,128)} fusion(bf16[2,4,128,5120]{3,2,1,0:T(8,128)(2,1)} %bitcast.57, bf16[64,2,4,128]{3,2,1,0:T(4,128)(2,1)S(1)} %fusion.44), kind=kOutput, calls=%fused_computation.13 | convolution fusion | flops 671088640 | bytes 11927552 | tf_op jit(solution)/shard_map/bkgc,kgcd->bd/dot_general | solution.py:70
  184.4 0.0 all-reduce.5.cloned.1.call-update
  184.4 33.9 %all-reduce.5.cloned.1.call-done = f32[64,5120]{1,0:T(8,128)} async-done(((f32[64,5120]{1,0:T(8,128)}), f32[64,5120]{1,0:T(8,128)}) %all-reduce.5.cloned.1.call-update) | async-done | bytes 1310736 | tf_op jit(solution)/shard_map/psum | solution.py:71
  218.3 3.7 %add_convert_fusion = bf16[64,5120]{1,0:T(8,128)(2,1)} fusion(f32[64,5120]{1,0:T(8,128)} %all-reduce.5.cloned.1.call-done, f32[]{:T(128)} %bitcast.12, f32[]{:T(128)} %bitcast, f32[5120]{0:T(1024)S(1)} %copy-done.2, f32[64]{0:T(128)S(1)} %add_rsqrt_fusion, bf16[64,5120]{1,0:T(8,128)(2,1)S(1)} %get-tuple-element.5), kind=kLoop, calls=%fused_computation.28 | loop fusion | flops 2949120 | bytes 2642184 | tf_op jit(solution)/shard_map/convert_element_type | solution.py:72
  (24 shorter events, 0.2 us)
Async XLA Ops:
  7.2 116.1 %all-reduce.3.cloned.1.call-start = ((), (), s32[]{:S(2)}) async-start(), calls=%async_computation | async-start | bytes 2621440 | tf_op jit(solution)/shard_map/psum | solution.py:54
  48.0 28.2 %copy-start = (bf16[64,5120]{1,0:T(8,128)(2,1)S(1)}, bf16[64,5120]{1,0:T(8,128)(2,1)}, u32[]{:S(2)}) copy-start(bf16[64,5120]{1,0:T(8,128)(2,1)} %param.16) | copy-start | bytes 1966084
  48.0 28.2 %copy-start.1 = (f32[5120]{0:T(1024)S(1)}, f32[5120]{0:T(1024)}, u32[]{:S(2)}) copy-start(f32[5120]{0:T(1024)} %param.21) | copy-start | bytes 61444
  48.0 28.2 %copy-start.6 = (f32[8,128]{1,0:T(8,128)S(1)}, f32[8,128]{1,0:T(8,128)}, u32[]{:S(2)}) copy-start(f32[8,128]{1,0:T(8,128)} %param.25) | copy-start | bytes 12292
  82.3 7.2 %copy-start.5 = (s32[64]{0:T(128)S(1)}, s32[64]{0:T(128)}, u32[]{:S(2)}) copy-start(s32[64]{0:T(128)} %param.17) | copy-start | bytes 772
  82.3 7.2 %copy-start.3 = (f32[2]{0:T(128)S(1)}, f32[2]{0:T(128)}, u32[]{:S(2)}) copy-start(f32[2]{0:T(128)} %param.30) | copy-start | bytes 28
  82.3 7.8 %copy-start.4 = (f32[2]{0:T(128)S(1)}, f32[2]{0:T(128)}, u32[]{:S(2)}) copy-start(f32[2]{0:T(128)} %param.31) | copy-start | bytes 28
  82.3 44.1 %copy-start.2 = (f32[5120]{0:T(1024)S(1)}, f32[5120]{0:T(1024)}, u32[]{:S(2)}) copy-start(f32[5120]{0:T(1024)} %param.27) | copy-start | bytes 61444
  89.4 128.9 %all-reduce.5.cloned.1.call-start = ((), (), s32[]{:S(2)}) async-start(), calls=%async_computation.1 | async-start | bytes 2621440 | tf_op jit(solution)/shard_map/psum | solution.py:71
Sparse Core Ops, SparseCore 0:
  89.5 33.7 all-reduce.2
  184.5 33.6 all-reduce.4
where the time goes:
time: 229 us
  matrix products  82 us (36%)
  waiting for transfers between devices  66.1 us (29%)
  other arithmetic  55.6 us (24%)
  between operations  14.3 us (6%)
  blocking collectives  8.93 us (4%)
    psum x1, waiting for transfers between devices, local_step(): attn_out = lax.psum(attn_part, 'tp')  33.9 us
    psum x1, waiting for transfers between devices, local_step(): lin_out = lax.psum(lin_part, 'tp')  32.3 us
    select_n x1, other arithmetic, local_step(): k_out = jnp.where(write_mask, key_new, k_cache)  23.1 us
    add x1, other arithmetic, local_step(): decay_rate * lin_state  22.7 us
    dot_general x1, matrix products, local_step(): jnp.einsum('bhk,bhkv->bhv', proj_lin[:, 0].astype(jnp.float32), state_out...  19.1 us
    dot_general x1, matrix products, local_step(): jnp.einsum('bd,dchk->bchk', h_first, w_qkv, preferred_element_type=jnp.fl...  15.7 us
    sub x1, matrix products, local_step(): jax.nn.softmax(jnp.where(valid_mask, scores, -jnp.inf), axis=-1)  10.4 us
    dot_general x1, matrix products, local_step(): jnp.einsum('bd,dkjc->bkjc', h_second, w_attn, preferred_element_type=jnp....  9.63 us
  transfers between devices with their start and end apart: 2, of which 2 were waited for; matrix products, arithmetic and copies ran while one was open for 1% of the time, Pallas kernels for 0%

commit v1 on v0

v1 whole, which is shorter than its diff:
```python
import functools
import jax
import jax.numpy as jnp
from jax import lax
from jax.experimental import pallas as pl
from jax.experimental.pallas import tpu as pltpu
from jax.sharding import PartitionSpec as P

EPS = 1e-5
ROPE_BASE = 10000000.0
F32 = jnp.float32
BF16 = jnp.bfloat16
MESH = pl.DeviceIdType.MESH
ANY = pl.BlockSpec(memory_space=pl.ANY)
VMEM = pl.BlockSpec(memory_space=pltpu.VMEM)
SMEM = pl.BlockSpec(memory_space=pltpu.SMEM)

DC = 256
RS = 9 * DC + 16
NWB = 4
NSB = 16
LAG = 4


def k1_body(hid, g1, wqkv, wgate, slopes, lin, st_out, o_out, gate_out, h1_out,
            wbuf, gbuf, scr, acc, qt, kt, vv, sbuf, wsem, rsem, ssem):
    nchunk = hid.shape[1] // DC

    def wcopies(i, slot):
        return (pltpu.make_async_copy(wqkv.at[pl.ds(i * (DC * 24), DC * 24)], wbuf.at[slot], wsem.at[slot, 0]),
                pltpu.make_async_copy(wgate.at[pl.ds(i * (DC * 8), DC * 8)], gbuf.at[slot], wsem.at[slot, 1]))

    def sread(j, slot):
        hp, bb = j // 8, lax.rem(j, 8)
        return pltpu.make_async_copy(lin.at[pl.ds(bb * 8, 8), pl.ds(hp * 2, 2)], sbuf.at[slot], rsem.at[slot])

    def swrite(j, slot):
        hp, bb = j // 8, lax.rem(j, 8)
        return pltpu.make_async_copy(sbuf.at[slot], st_out.at[pl.ds(bb * 8, 8), pl.ds(hp * 2, 2)], ssem.at[slot])

    for i in range(NWB):
        for c in wcopies(i, i):
            c.start()
    x = hid[...].astype(F32)
    h1_out[...] = (x * lax.rsqrt(jnp.mean(x * x, axis=-1, keepdims=True) + EPS) * g1[...]).astype(BF16)
    acc[...] = jnp.zeros_like(acc)

    def wstep(i, carry):
        slot = lax.rem(i, NWB)
        for c in wcopies(i, slot):
            c.wait()
        for d2 in range(0, DC, 2):
            t = wbuf[slot, pl.ds(d2 * 24, 48)].astype(F32)
            for u in range(6):
                scr[pl.ds((u % 3) * RS + 9 * (d2 + u // 3), 8, stride=2)] = t[u * 8:(u + 1) * 8]
            t = gbuf[slot, pl.ds(d2 * 8, 16)].astype(F32)
            for u in range(2):
                scr[pl.ds(3 * RS + 9 * (d2 + u), 8, stride=2)] = t[u * 8:(u + 1) * 8]
        hh = h1_out[:, pl.ds(pl.multiple_of(i * DC, DC), DC)]

        def head(m):
            return scr[pl.ds((m // 8) * RS + 2 * (m % 8), DC, stride=9)]

        for n in range(16):
            r = jnp.concatenate([head(2 * n), head(2 * n + 1)], axis=1).astype(BF16)
            acc[:, n * 256:(n + 1) * 256] += jnp.dot(hh, r, preferred_element_type=F32)

        @pl.when(i + NWB < nchunk)
        def _():
            for c in wcopies(i + NWB, slot):
                c.start()

        @pl.when(i < NSB)
        def _():
            sread(i, i).start()
        return carry

    lax.fori_loop(0, nchunk, wstep, 0)

    for hp in range(4):
        def pair(c):
            base = c * 1024 + hp * 256
            return jnp.concatenate([acc[:, base:base + 128], acc[:, base + 128:base + 256]], axis=0)

        def act(c):
            z = pair(c)
            return (z * jax.nn.sigmoid(z)).astype(BF16).astype(F32)
        qt[hp] = act(0).T
        kt[hp] = act(1).T
        vv[hp] = act(2)
        g = jax.nn.sigmoid(pair(3))
        gate_out[2 * hp] = g[:64]
        gate_out[2 * hp + 1] = g[64:]

    def sstep(j, carry):
        hp, bb = j // 8, lax.rem(j, 8)
        slot = lax.rem(j, NSB)
        sread(j, slot).wait()
        shift = lax.rem(128 - bb * 8, 128)
        qr = pltpu.roll(qt[hp], shift, 1)
        kr = pltpu.roll(kt[hp], shift, 1)
        for p in range(2):
            decay = jnp.exp(jnp.full((8, 128), -slopes[hp * 2 + p], F32))[0:1]
            vrows = vv[hp, pl.ds(p * 64 + bb * 8, 8)]
            rows = []
            for i in range(8):
                col = p * 64 + i
                kc = jnp.broadcast_to(kr[:, col:col + 1], (128, 128))
                qc = jnp.broadcast_to(qr[:, col:col + 1], (128, 128))
                s_new = decay * sbuf[slot, i, p] + kc * vrows[i:i + 1]
                sbuf[slot, i, p] = s_new
                rows.append(jnp.sum(qc * s_new, axis=0, keepdims=True))
            o_out[hp * 2 + p, pl.ds(bb * 8, 8)] = jnp.concatenate(rows, axis=0)
        swrite(j, slot).start()

        @pl.when((j >= LAG) & (j - LAG + NSB < 32))
        def _():
            jj = j - LAG
            ps = lax.rem(jj, NSB)
            swrite(jj, ps).wait()
            sread(jj + NSB, ps).start()
        return carry

    lax.fori_loop(0, 32, sstep, 0)
    for j in range(32 - NSB, 32):
        swrite(j, j % NSB).wait()


def k1(hidden, g1, wqkv, wgate, slopes, lin):
    return pl.pallas_call(
        k1_body,
        out_shape=(jax.ShapeDtypeStruct(lin.shape, F32), jax.ShapeDtypeStruct((8, 64, 128), F32),
                   jax.ShapeDtypeStruct((8, 64, 128), F32), jax.ShapeDtypeStruct(hidden.shape, BF16)),
        in_specs=[VMEM, VMEM, ANY, ANY, SMEM, ANY],
        out_specs=(ANY, VMEM, VMEM, VMEM),
        scratch_shapes=[
            pltpu.VMEM((NWB, DC * 24, 128), BF16), pltpu.VMEM((NWB, DC * 8, 128), BF16),
            pltpu.VMEM((4 * RS, 128), F32), pltpu.VMEM((64, 4096), F32),
            pltpu.VMEM((4, 128, 128), F32), pltpu.VMEM((4, 128, 128), F32), pltpu.VMEM((4, 128, 128), F32),
            pltpu.VMEM((NSB, 8, 2, 128, 128), F32),
            pltpu.SemaphoreType.DMA((NWB, 2)), pltpu.SemaphoreType.DMA((NSB,)), pltpu.SemaphoreType.DMA((NSB,))],
        compiler_params=pltpu.CompilerParams(vmem_limit_bytes=50 * 2 ** 20),
        name='lightning')(hidden, g1, wqkv, wgate, slopes, lin)


NCH = 5
CW = 512
HALF = NCH * CW


def entry_barrier():
    tp = lax.axis_index('tp')
    bar = pltpu.get_barrier_semaphore()
    for peer in peers(tp):
        pl.semaphore_signal(bar, inc=1, device_id={'tp': peer}, device_id_type=MESH)
    pl.semaphore_wait(bar, 3)


def peers(tp):
    core = lax.rem(tp, 2)
    partner = tp + 1 - 2 * core
    across = lax.rem(tp + 2, 4)
    diag = lax.rem(partner + 2, 4)
    return partner, across, diag


def out_weight_copies(w, wo, wosem):
    core = lax.rem(lax.axis_index('tp'), 2)
    out = []
    for s in range(2 * NCH):
        side = core if s % 2 else 1 - core
        col = pl.multiple_of(side * HALF + (s // 2) * CW, CW)
        out.append(pltpu.make_async_copy(w.at[:, pl.ds(col, CW)], wo.at[s], wosem.at[s]))
    return out


def reduce_over_tp(xin, wo, wcopies, full, send_a, recv_a, own, recv_x, sems, between):
    tp = lax.axis_index('tp')
    core = lax.rem(tp, 2)
    partner, across, _ = peers(tp)

    def rcopy(src, dst, k, j, dev):
        return pltpu.make_async_remote_copy(src_ref=src, dst_ref=dst, send_sem=sems.at[k, j],
                                            recv_sem=sems.at[k + 1, j], device_id={'tp': dev}, device_id_type=MESH)
    ca = [rcopy(send_a.at[j], recv_a.at[j], 0, j, partner) for j in range(NCH)]
    cx = [rcopy(own.at[j], recv_x.at[j], 2, j, across) for j in range(NCH)]
    cf = []
    for j in range(NCH):
        col = pl.multiple_of(core * HALF + j * CW, CW)
        cf.append(rcopy(full.at[:, pl.ds(col, CW)], full.at[:, pl.ds(col, CW)], 4, j, partner))

    def combine(j):
        ca[j].wait_recv()
        own[j] = own[j] + recv_a[j]
        cx[j].start()

    for j in range(NCH):
        wcopies[2 * j].wait()
        send_a[j] = jnp.dot(xin[...], wo[2 * j], preferred_element_type=F32)
        ca[j].start()
        wcopies[2 * j + 1].wait()
        own[j] = jnp.dot(xin[...], wo[2 * j + 1], preferred_element_type=F32)
        if j:
            combine(j - 1)
    combine(NCH - 1)
    for j in range(NCH):
        between(j)
        cx[j].wait_recv()
        col = pl.multiple_of(core * HALF + j * CW, CW)
        full[:, pl.ds(col, CW)] = own[j] + recv_x[j]
        cf[j].start()
    for j in range(NCH):
        cf[j].wait_recv()
    for j in range(NCH):
        ca[j].wait_send()
        cx[j].wait_send()
        cf[j].wait_send()


REDUCE_SCRATCH = [
    pltpu.VMEM((64, 2 * HALF), F32), pltpu.VMEM((NCH, 64, CW), F32), pltpu.VMEM((NCH, 64, CW), F32),
    pltpu.VMEM((NCH, 64, CW), F32), pltpu.VMEM((NCH, 64, CW), F32),
    pltpu.VMEM((2 * NCH, 1024, CW), BF16), pltpu.SemaphoreType.DMA((6, NCH)), pltpu.SemaphoreType.DMA((2 * NCH,))]

NAB = 4


def k2_body(o_in, gate_in, h1, onorm, w_out, g2, wattn, cosf, sina, sinb, alpha, beta,
            h2_out, qs, kn, vn,
            full, send_a, recv_a, own, recv_x, wo, sems, wosem,
            xin, ssl, ssr, sssem, abuf, ascr, wd, asem):
    tp = lax.axis_index('tp')
    nchunk = h1.shape[1] // DC
    wcopies = out_weight_copies(w_out, wo, wosem)
    for c in wcopies:
        c.start()

    def acopy(i, slot):
        return pltpu.make_async_copy(wattn.at[pl.ds(i * (DC * 12), DC * 12)], abuf.at[slot], asem.at[slot])
    for i in range(NAB):
        acopy(i, i).start()
    sq = jnp.zeros((64, 128), F32)
    for h in range(8):
        sq = sq + o_in[h] * o_in[h]
    ssl[...] = sq
    entry_barrier()
    copies = [pltpu.make_async_remote_copy(src_ref=ssl, dst_ref=ssr.at[k], send_sem=sssem.at[0, k],
                                           recv_sem=sssem.at[1, k], device_id={'tp': dev}, device_id_type=MESH)
              for k, dev in enumerate(peers(tp))]
    for c in copies:
        c.start()
    for c in copies:
        c.wait_recv()
    total = jnp.sum((ssl[...] + ssr[0]) + (ssr[1] + ssr[2]), axis=-1, keepdims=True)
    inv = lax.rsqrt(total / 4096.0 + EPS)
    for h in range(8):
        xin[:, h * 128:(h + 1) * 128] = (o_in[h] * inv * onorm[h:h + 1] * gate_in[h]).astype(BF16)

    def demix(i, carry):
        slot = lax.rem(i, NAB)
        acopy(i, slot).wait()
        ascr[...] = abuf[slot].astype(F32)
        for j in range(6):
            for kv in range(2):
                wd[j, kv, pl.ds(pl.multiple_of(i * DC, DC), DC)] = ascr[pl.ds(2 * j + kv, DC, stride=12)].astype(BF16)

        @pl.when(i + NAB < nchunk)
        def _():
            acopy(i + NAB, slot).start()
        return carry

    def between(j):
        lax.fori_loop(j * (nchunk // NCH), (j + 1) * (nchunk // NCH), demix, 0)

    reduce_over_tp(xin, wo, wcopies, full, send_a, recv_a, own, recv_x, sems, between)
    for c in copies:
        c.wait_send()
    mid = (alpha[0] * h1[...].astype(F32) + beta[0] * full[...]).astype(BF16).astype(F32)
    h2_out[...] = (mid * lax.rsqrt(jnp.mean(mid * mid, axis=-1, keepdims=True) + EPS) * g2[...]).astype(BF16)
    qs[...] = jnp.zeros_like(qs)

    def turn(z):
        return z * cosf[...] + pltpu.roll(z, 96, 1) * sina[...] + pltpu.roll(z, 32, 1) * sinb[...]

    for j in range(6):
        r = jnp.concatenate([wd[j, 0], wd[j, 1]], axis=1)
        z = jnp.dot(h2_out[...], r, preferred_element_type=F32)
        for kv in range(2):
            zk = z[:, kv * 128:(kv + 1) * 128]
            if j < 4:
                qs[kv, pl.ds(kv * 4 + j, 64, stride=8)] = turn(zk).astype(BF16).astype(F32)
            elif j == 4:
                kn[kv] = turn(zk).astype(BF16).astype(F32)
            else:
                vn[kv] = zk.astype(BF16).astype(F32)


def k2(o, gate, h1, onorm, w_out, g2, wattn, cosf, sina, sinb, alpha, beta):
    return pl.pallas_call(
        k2_body,
        out_shape=(jax.ShapeDtypeStruct(h1.shape, BF16), jax.ShapeDtypeStruct((2, 512, 128), F32),
                   jax.ShapeDtypeStruct((2, 64, 128), F32), jax.ShapeDtypeStruct((2, 64, 128), F32)),
        in_specs=[VMEM, VMEM, VMEM, VMEM, ANY, VMEM, ANY, VMEM, VMEM, VMEM, SMEM, SMEM],
        out_specs=(VMEM, VMEM, VMEM, VMEM),
        scratch_shapes=REDUCE_SCRATCH + [
            pltpu.VMEM((64, 1024), BF16), pltpu.VMEM((64, 128), F32), pltpu.VMEM((3, 64, 128), F32),
            pltpu.SemaphoreType.DMA((2, 3)),
            pltpu.VMEM((NAB, DC * 12, 128), BF16), pltpu.VMEM((DC * 12, 128), F32),
            pltpu.VMEM((6, 2, h1.shape[1], 128), BF16), pltpu.SemaphoreType.DMA((NAB,))],
        compiler_params=pltpu.CompilerParams(vmem_limit_bytes=50 * 2 ** 20, collective_id=0, has_side_effects=True),
        name='mix_first')(o, gate, h1, onorm, w_out, g2, wattn, cosf, sina, sinb, alpha, beta)


NB3 = 4
NS3 = 5


def k3_body(kc, vc, qs, kn, vn, clen, k_out, v_out, attn, kb, vb, rsem, wsem):
    nstep = kc.shape[0] // NB3

    def reads(i, slot):
        return (pltpu.make_async_copy(kc.at[pl.ds(i * NB3, NB3)], kb.at[slot], rsem.at[slot, 0]),
                pltpu.make_async_copy(vc.at[pl.ds(i * NB3, NB3)], vb.at[slot], rsem.at[slot, 1]))

    def writes(i, slot):
        return (pltpu.make_async_copy(kb.at[slot], k_out.at[pl.ds(i * NB3, NB3)], wsem.at[slot, 0]),
                pltpu.make_async_copy(vb.at[slot], v_out.at[pl.ds(i * NB3, NB3)], wsem.at[slot, 1]))

    for i in range(NS3 - 1):
        for c in reads(i, i):
            c.start()

    def step(i, carry):
        slot = lax.rem(i, NS3)
        for c in reads(i, slot):
            c.wait()
        row_id = lax.broadcasted_iota(jnp.int32, (16, 128), 0)
        for u in range(NB3):
            b = i * NB3 + u
            pos = clen[b]
            base = pl.multiple_of((pos // 16) * 16, 16)
            hit = row_id == pos - base
            for kv in range(2):
                for buf, new in ((kb, kn), (vb, vn)):
                    old = buf[slot, u, kv, pl.ds(base, 16)].astype(F32)
                    row = jnp.broadcast_to(new[kv, pl.ds(b, 1)], (16, 128))
                    buf[slot, u, kv, pl.ds(base, 16)] = jnp.where(hit, row, old).astype(BF16)
        for c in writes(i, slot):
            c.start()
        tpos = lax.broadcasted_iota(jnp.int32, (8, 512), 1)
        lo = lax.broadcasted_iota(jnp.int32, (8, 128), 0) < 4
        for u in range(NB3):
            b = i * NB3 + u
            q = jnp.concatenate([qs[0, pl.ds(b * 8, 8)], qs[1, pl.ds(b * 8, 8)]], axis=1).astype(BF16)
            kk = jnp.concatenate([kb[slot, u, 0], kb[slot, u, 1]], axis=1)
            vvv = jnp.concatenate([vb[slot, u, 0], vb[slot, u, 1]], axis=1)
            s = lax.dot_general(q, kk, (((1,), (1,)), ((), ())), preferred_element_type=F32) * (128 ** -0.5)
            s = jnp.where(tpos <= clen[b], s, -jnp.inf)
            e = jnp.exp(s - jnp.max(s, axis=-1, keepdims=True))
            pr = (e / jnp.sum(e, axis=-1, keepdims=True)).astype(BF16)
            r = jnp.dot(pr, vvv, preferred_element_type=F32)
            attn[pl.ds(b * 8, 8)] = jnp.where(lo, r[:, :128], r[:, 128:]).astype(BF16).astype(F32)

        nxt = i + NS3 - 1

        @pl.when(nxt < nstep)
        def _():
            ps = lax.rem(nxt, NS3)

            @pl.when(i >= 1)
            def _():
                for c in writes(i - 1, ps):
                    c.wait()
            for c in reads(nxt, ps):
                c.start()
        return carry

    lax.fori_loop(0, nstep, step, 0)
    for i in range(nstep - NS3, nstep):
        for c in writes(i, i % NS3):
            c.wait()


def k3(kc, vc, qs, kn, vn, clen):
    shape = (NS3, NB3) + kc.shape[1:]
    return pl.pallas_call(
        k3_body,
        out_shape=(jax.ShapeDtypeStruct(kc.shape, BF16), jax.ShapeDtypeStruct(vc.shape, BF16),
                   jax.ShapeDtypeStruct((512, 128), F32)),
        in_specs=[ANY, ANY, VMEM, VMEM, VMEM, SMEM],
        out_specs=(ANY, ANY, VMEM),
        scratch_shapes=[pltpu.VMEM(shape, BF16), pltpu.VMEM(shape, BF16),
                        pltpu.SemaphoreType.DMA((NS3, 2)), pltpu.SemaphoreType.DMA((NS3, 2))],
        compiler_params=pltpu.CompilerParams(vmem_limit_bytes=50 * 2 ** 20),
        name='attention')(kc, vc, qs, kn, vn, clen)


def k4_body(attn, h2, w_out, alpha, beta, out,
            full, send_a, recv_a, own, recv_x, wo, sems, wosem, xin):
    wcopies = out_weight_copies(w_out, wo, wosem)
    for c in wcopies:
        c.start()
    for r in range(8):
        xin[:, r * 128:(r + 1) * 128] = attn[pl.ds(r, 64, stride=8)].astype(BF16)
    entry_barrier()
    reduce_over_tp(xin, wo, wcopies, full, send_a, recv_a, own, recv_x, sems, lambda j: None)
    out[...] = (alpha[1] * h2[...].astype(F32) + beta[1] * full[...]).astype(BF16)


def k4(attn, h2, w_out, alpha, beta):
    return pl.pallas_call(
        k4_body,
        out_shape=jax.ShapeDtypeStruct(h2.shape, BF16),
        in_specs=[VMEM, VMEM, ANY, SMEM, SMEM],
        out_specs=VMEM,
        scratch_shapes=REDUCE_SCRATCH + [pltpu.VMEM((64, 1024), BF16)],
        compiler_params=pltpu.CompilerParams(vmem_limit_bytes=50 * 2 ** 20, collective_id=1, has_side_effects=True),
        name='mix_second')(attn, h2, w_out, alpha, beta)


def rope_tables(clen):
    inv_freq = ROPE_BASE ** (-2.0 * jnp.arange(32, dtype=F32) / 64)
    ang = clen.astype(F32)[:, None] * inv_freq[None, :]
    cos, sin = jnp.cos(ang), jnp.sin(ang)
    zero = jnp.zeros((clen.shape[0], 32), F32)
    one = jnp.ones((clen.shape[0], 64), F32)
    cosf = jnp.concatenate([cos, cos, one], axis=1)
    sina = jnp.concatenate([-sin, zero, zero, zero], axis=1)
    sinb = jnp.concatenate([zero, sin, zero, zero], axis=1)
    return cosf, sina, sinb


def solution(mesh):
    row_spec = P('dp', None)
    cache_spec = P('dp', 'tp', None, None)
    in_specs = (row_spec, P('dp'), cache_spec, cache_spec, cache_spec, P(None), P(None, None, 'tp', None),
                P(None, 'tp', None), P('tp'), P('tp', None), P('tp', None, None), P(None),
                P(None, 'tp', None, None), P('tp', None, None), P(None), P(None))
    out_specs = (row_spec, cache_spec, cache_spec, cache_spec)

    def local_step(hidden, cache_len, lin_state, k_cache, v_cache, norm_first, w_qkv, w_gate, slopes, out_norm,
                   w_out_lin, norm_second, w_attn, w_out_attn, mix_alpha, mix_beta):
        d = hidden.shape[1]
        cosf, sina, sinb = rope_tables(cache_len)
        state_out, o, gate, h1 = k1(hidden, norm_first.reshape(1, d), w_qkv.reshape(-1, 128),
                                    w_gate.reshape(-1, 128), slopes, lin_state)
        wattn = jnp.transpose(w_attn, (0, 2, 1, 3)).reshape(-1, 128)
        h2, qs, kn, vn = k2(o, gate, h1, out_norm, w_out_lin.reshape(-1, d), norm_second.reshape(1, d), wattn,
                            cosf, sina, sinb, mix_alpha, mix_beta)
        k_out, v_out, attn = k3(k_cache, v_cache, qs, kn, vn, cache_len)
        hidden_out = k4(attn, h2, w_out_attn.reshape(-1, d), mix_alpha, mix_beta)
        return hidden_out, state_out, k_out, v_out

    return jax.shard_map(local_step, mesh=mesh, in_specs=in_specs, out_specs=out_specs, check_vma=False)
```

time: 229 us -> 130 us (0.57)
  Pallas kernels: 0 us -> 125 us
  matrix products: 82 us -> 0 us
  waiting for transfers between devices: 66.1 us -> 0 us
  other arithmetic: 55.6 us -> 0.96 us
  between operations: 14.3 us -> 0.75 us
  blocking collectives: 8.93 us -> 0 us
    pallas_call x0 -> x4, Pallas kernels: none -> 125 us  [the longest x1 44 us: k1(): pl.pallas_call(k1_body, out_shape=(jax.ShapeDtypeStruct(lin.shape, F32),...]
    dot_general x7 -> x0, matrix products: 71.6 us -> none  [the longest x1 19.1 us: local_step(): jnp.einsum('bhk,bhkv->bhv', proj_lin[:, 0].astype(jnp.float32), state_out...]
    psum x2 -> x0, waiting for transfers between devices: 66.1 us -> none  [the longest x1 33.9 us: local_step(): attn_out = lax.psum(attn_part, 'tp')]
    select_n x1 -> x0, other arithmetic: 23.1 us -> none  [local_step(): k_out = jnp.where(write_mask, key_new, k_cache)]
    add x1 -> x0, other arithmetic: 22.7 us -> none  [local_step(): decay_rate * lin_state]
    sub x1 -> x0, matrix products: 10.4 us -> none  [local_step(): jax.nn.softmax(jnp.where(valid_mask, scores, -jnp.inf), axis=-1)]
    psum x1 -> x0, blocking collectives: 8.93 us -> none  [local_step(): sq_sum = lax.psum(jnp.sum(lin_attn * lin_attn, axis=(1, 2)), 'tp')]
    reduce_sum x3 -> x0, other arithmetic: 4.58 us -> none  [the longest x2 4.44 us: rms_scale(): jnp.mean(wide_vals * wide_vals, axis=-1, keepdims=True) + EPS]
  transfers between devices with their start and end apart: 2 -> 0, of which waited for: 2 -> 0; matrix products, arithmetic and copies ran while one was open for 1% -> 0% of each run, Pallas kernels for 0% -> 0%
where the time goes in v1:
time: 130 us
  Pallas kernels  125 us (96%)
  local copies, waits for them, and re-layouts  3.5 us (3%)
    pallas_call x1, Pallas kernels, k1(): pl.pallas_call(k1_body, out_shape=(jax.ShapeDtypeStruct(lin.shape, F32),...  44 us
    pallas_call x1, Pallas kernels, k3(): pl.pallas_call(k3_body, out_shape=(jax.ShapeDtypeStruct(kc.shape, BF16),...  30.5 us
    pallas_call x1, Pallas kernels, k2(): pl.pallas_call(k2_body, out_shape=(jax.ShapeDtypeStruct(h1.shape, BF16),...  29.5 us
    pallas_call x1, Pallas kernels, k4(): pl.pallas_call(k4_body, out_shape=jax.ShapeDtypeStruct(h2.shape, BF16), i...  20.7 us
    unnamed x17, local copies, waits for them, and re-layouts  3.32 us

profile of v1, /device:TPU:0, one launch (start us, length us, event | category | flops | bytes accessed | tf_op | source)
XLA Modules:
  0.0 129.9 jit_solution(2963854795970086938)
XLA Ops:
  0.6 0.7 convert_element_type.3
  1.3 0.1 pad.6.clone
  1.4 0.1 pad.3.clone
  1.5 0.2 multiply_sine_fusion
  1.7 0.1 maximum_maximum_fusion
  1.8 0.0 copy-start
  1.8 1.1 copy-done
  2.9 0.0 copy-start.1
  2.9 0.7 copy-done.1
  3.6 0.0 copy-start.6
  3.6 0.7 copy-done.6
  4.3 0.0 copy-start.2
  4.3 0.0 copy-start.3
  4.3 0.0 copy-start.4
  4.3 0.0 copy-start.5
  4.3 44.0 %lightning.1 = (f32[64,8,128,128]{3,2,1,0:T(8,128)}, f32[8,64,128]{2,1,0:T(8,128)S(1)}, f32[8,64,128]{2,1,0:T(8,128)S(1)}, bf16[64,5120]{1,0:T(8,128)(2,1)S(1)}) custom-call(bf16[64,5120]{1,0:T(8,128)(2,1)S(1)} %copy-done, f32[1,5120]{1,0:T(1,128)S(1)} %bitcast.9, bf16[122880,128]{1,0:T(8,128)(2,1)} %bitcast.11, bf16[40960,128]{1,0:T(8,128)(2,1)} %bitcast.13, ...), custom_call_target="tpu_custom_call" | custom-call | tf_op jit(solution)/shard_map/lightning/pallas_call | solution.py:130
  48.3 0.0 copy-start.7
  48.3 0.0 copy-done.2
  48.3 0.0 copy-done.3
  48.3 0.0 copy-done.4
  48.3 0.0 copy-done.5
  48.3 29.5 %mix_first.1 = (bf16[64,5120]{1,0:T(8,128)(2,1)S(1)}, f32[2,512,128]{2,1,0:T(8,128)S(1)}, f32[2,64,128]{2,1,0:T(8,128)S(1)}, f32[2,64,128]{2,1,0:T(8,128)S(1)}) custom-call(f32[8,64,128]{2,1,0:T(8,128)S(1)} %get-tuple-element.15.o_in, f32[8,64,128]{2,1,0:T(8,128)S(1)} %get-tuple-element.16.gate_in, bf16[64,5120]{1,0:T(8,128)(2,1)S(1)} %get-tuple-element.17.h1, ...), custom_call_target="tpu_custom_call" | custom-call | tf_op jit(solution)/shard_map/mix_first/pallas_call | solution.py:299
  77.8 0.0 copy-done.7
  77.8 30.5 %attention.1 = (bf16[64,2,512,128]{3,2,1,0:T(8,128)(2,1)}, bf16[64,2,512,128]{3,2,1,0:T(8,128)(2,1)}, f32[512,128]{1,0:T(8,128)S(1)}) custom-call(bf16[64,2,512,128]{3,2,1,0:T(8,128)(2,1)} %kc.1, bf16[64,2,512,128]{3,2,1,0:T(8,128)(2,1)} %vc.1, f32[2,512,128]{2,1,0:T(8,128)S(1)} %get-tuple-element.18.qs, f32[2,64,128]{2,1,0:T(8,128)S(1)} %get-tuple-element.19.kn, ...), custom_call_target="tpu_custom_call" | custom-call | tf_op jit(solution)/shard_map/attention/pallas_call | solution.py:386
  108.3 20.7 %mix_second.1 = bf16[64,5120]{1,0:T(8,128)(2,1)S(1)} custom-call(f32[512,128]{1,0:T(8,128)S(1)} %get-tuple-element.21.attn, bf16[64,5120]{1,0:T(8,128)(2,1)S(1)} %get-tuple-element.22.h2, bf16[1024,5120]{1,0:T(8,128)(2,1)} %bitcast.15, f32[2]{0:T(128)S(1)} %copy-done.4, f32[2]{0:T(128)S(1)} %copy-done.5), custom_call_target="tpu_custom_call" | custom-call | tf_op jit(solution)/shard_map/mix_second/pallas_call | solution.py:411
  129.1 0.8 copy.21
  (6 shorter events, 0.0 us)
Async XLA Ops:
  1.8 1.1 copy-start
  2.9 0.7 copy-start.1
  3.6 0.7 copy-start.6
  4.3 44.0 %copy-start.2 = (f32[5120]{0:T(1024)S(1)}, f32[5120]{0:T(1024)}, u32[]{:S(2)}) copy-start(f32[5120]{0:T(1024)} %param.27) | copy-start | bytes 61444
  4.3 44.0 %copy-start.3 = (f32[8,128]{1,0:T(8,128)S(1)}, f32[8,128]{1,0:T(8,128)}, u32[]{:S(2)}) copy-start(f32[8,128]{1,0:T(8,128)} %onorm.1) | copy-start | bytes 12292
  4.3 44.0 %copy-start.4 = (f32[2]{0:T(128)S(1)}, f32[2]{0:T(128)}, u32[]{:S(2)}) copy-start(f32[2]{0:T(128)} %alpha.3) | copy-start | bytes 28
  4.3 44.0 %copy-start.5 = (f32[2]{0:T(128)S(1)}, f32[2]{0:T(128)}, u32[]{:S(2)}) copy-start(f32[2]{0:T(128)} %beta.3) | copy-start | bytes 28
  48.3 29.6 %copy-start.7 = (s32[64]{0:T(128)S(1)}, s32[64]{0:T(128)}, u32[]{:S(2)}) copy-start(s32[64]{0:T(128)} %clen.1) | copy-start | bytes 772

commit v2 on v1

--- a/solution.py
+++ b/solution.py
@@ -22,9 +22,13 @@
 LAG = 4
 
 
-def k1_body(hid, g1, wqkv, wgate, slopes, lin, st_out, o_out, gate_out, h1_out,
-            wbuf, gbuf, scr, acc, qt, kt, vv, sbuf, wsem, rsem, ssem):
+def k1_body(hid_hbm, g1_hbm, wqkv, wgate, slopes_hbm, lin, st_out, o_out, gate_out, h1_out,
+            wbuf, gbuf, scr, acc, qq, kk, vv, sbuf, hid, g1, slopes, wsem, rsem, ssem, msem):
     nchunk = hid.shape[1] // DC
+    small = [pltpu.make_async_copy(src, dst, msem.at[n])
+             for n, (src, dst) in enumerate(((hid_hbm, hid), (g1_hbm, g1), (slopes_hbm, slopes)))]
+    for c in small:
+        c.start()
 
     def wcopies(i, slot):
         return (pltpu.make_async_copy(wqkv.at[pl.ds(i * (DC * 24), DC * 24)], wbuf.at[slot], wsem.at[slot, 0]),
@@ -41,6 +45,8 @@
     for i in range(NWB):
         for c in wcopies(i, i):
             c.start()
+    for c in small:
+        c.wait()
     x = hid[...].astype(F32)
     h1_out[...] = (x * lax.rsqrt(jnp.mean(x * x, axis=-1, keepdims=True) + EPS) * g1[...]).astype(BF16)
     acc[...] = jnp.zeros_like(acc)
@@ -85,8 +91,8 @@
         def act(c):
             z = pair(c)
             return (z * jax.nn.sigmoid(z)).astype(BF16).astype(F32)
-        qt[hp] = act(0).T
-        kt[hp] = act(1).T
+        qq[hp] = act(0)
+        kk[hp] = act(1)
         vv[hp] = act(2)
         g = jax.nn.sigmoid(pair(3))
         gate_out[2 * hp] = g[:64]
@@ -96,20 +102,19 @@
         hp, bb = j // 8, lax.rem(j, 8)
         slot = lax.rem(j, NSB)
         sread(j, slot).wait()
-        shift = lax.rem(128 - bb * 8, 128)
-        qr = pltpu.roll(qt[hp], shift, 1)
-        kr = pltpu.roll(kt[hp], shift, 1)
+        rid = lax.broadcasted_iota(jnp.int32, (16, 128), 0)
         for p in range(2):
             decay = jnp.exp(jnp.full((8, 128), -slopes[hp * 2 + p], F32))[0:1]
-            vrows = vv[hp, pl.ds(p * 64 + bb * 8, 8)]
+            at = pl.ds(p * 64 + bb * 8, 8)
+            kq = jnp.concatenate([kk[hp, at], qq[hp, at]], axis=0).T.astype(BF16)
+            v16 = jnp.concatenate([vv[hp, at], jnp.zeros((8, 128), F32)], axis=0)
             rows = []
             for i in range(8):
-                col = p * 64 + i
-                kc = jnp.broadcast_to(kr[:, col:col + 1], (128, 128))
-                qc = jnp.broadcast_to(qr[:, col:col + 1], (128, 128))
-                s_new = decay * sbuf[slot, i, p] + kc * vrows[i:i + 1]
+                pick = jnp.concatenate([jnp.where(rid == i, v16, 0.0), jnp.where(rid == 8 + i, 1.0, 0.0)], axis=1)
+                both = jnp.dot(kq, pick.astype(BF16), preferred_element_type=F32)
+                s_new = decay * sbuf[slot, i, p] + both[:, :128]
                 sbuf[slot, i, p] = s_new
-                rows.append(jnp.sum(qc * s_new, axis=0, keepdims=True))
+                rows.append(jnp.sum(both[:, 128:] * s_new, axis=0, keepdims=True))
             o_out[hp * 2 + p, pl.ds(bb * 8, 8)] = jnp.concatenate(rows, axis=0)
         swrite(j, slot).start()
 
@@ -131,14 +136,16 @@
         k1_body,
         out_shape=(jax.ShapeDtypeStruct(lin.shape, F32), jax.ShapeDtypeStruct((8, 64, 128), F32),
                    jax.ShapeDtypeStruct((8, 64, 128), F32), jax.ShapeDtypeStruct(hidden.shape, BF16)),
-        in_specs=[VMEM, VMEM, ANY, ANY, SMEM, ANY],
+        in_specs=[ANY] * 6,
         out_specs=(ANY, VMEM, VMEM, VMEM),
         scratch_shapes=[
             pltpu.VMEM((NWB, DC * 24, 128), BF16), pltpu.VMEM((NWB, DC * 8, 128), BF16),
             pltpu.VMEM((4 * RS, 128), F32), pltpu.VMEM((64, 4096), F32),
             pltpu.VMEM((4, 128, 128), F32), pltpu.VMEM((4, 128, 128), F32), pltpu.VMEM((4, 128, 128), F32),
             pltpu.VMEM((NSB, 8, 2, 128, 128), F32),
-            pltpu.SemaphoreType.DMA((NWB, 2)), pltpu.SemaphoreType.DMA((NSB,)), pltpu.SemaphoreType.DMA((NSB,))],
+            pltpu.VMEM(hidden.shape, BF16), pltpu.VMEM(g1.shape, F32), pltpu.SMEM(slopes.shape, F32),
+            pltpu.SemaphoreType.DMA((NWB, 2)), pltpu.SemaphoreType.DMA((NSB,)), pltpu.SemaphoreType.DMA((NSB,)),
+            pltpu.SemaphoreType.DMA((3,))],
         compiler_params=pltpu.CompilerParams(vmem_limit_bytes=50 * 2 ** 20),
         name='lightning')(hidden, g1, wqkv, wgate, slopes, lin)
 
@@ -311,11 +318,11 @@
         name='mix_first')(o, gate, h1, onorm, w_out, g2, wattn, cosf, sina, sinb, alpha, beta)
 
 
-NB3 = 4
-NS3 = 5
-
-
-def k3_body(kc, vc, qs, kn, vn, clen, k_out, v_out, attn, kb, vb, rsem, wsem):
+NB3 = 8
+NS3 = 4
+
+
+def k3_body(kc, vc, qs, kn, vn, clen, k_out, v_out, attn, kb, vb, sscr, rsem, wsem):
     nstep = kc.shape[0] // NB3
 
     def reads(i, slot):
@@ -347,20 +354,35 @@
                     buf[slot, u, kv, pl.ds(base, 16)] = jnp.where(hit, row, old).astype(BF16)
         for c in writes(i, slot):
             c.start()
+
+        def score(h, carry):
+            for u in range(NB3 // 2):
+                w = h * (NB3 // 2) + u
+                b = i * NB3 + w
+                q = jnp.concatenate([qs[0, pl.ds(b * 8, 8)], qs[1, pl.ds(b * 8, 8)]], axis=1).astype(BF16)
+                both = jnp.concatenate([kb[slot, w, 0], kb[slot, w, 1]], axis=1)
+                s = lax.dot_general(q, both, (((1,), (1,)), ((), ())), preferred_element_type=F32)
+                sscr[w] = s * (128 ** -0.5)
+            return carry
+
+        lax.fori_loop(0, 2, score, 0)
         tpos = lax.broadcasted_iota(jnp.int32, (8, 512), 1)
+        for w in range(NB3):
+            s = jnp.where(tpos <= clen[i * NB3 + w], sscr[w], -jnp.inf)
+            e = jnp.exp(s - jnp.max(s, axis=-1, keepdims=True))
+            sscr[w] = (e / jnp.sum(e, axis=-1, keepdims=True)).astype(BF16).astype(F32)
         lo = lax.broadcasted_iota(jnp.int32, (8, 128), 0) < 4
-        for u in range(NB3):
-            b = i * NB3 + u
-            q = jnp.concatenate([qs[0, pl.ds(b * 8, 8)], qs[1, pl.ds(b * 8, 8)]], axis=1).astype(BF16)
-            kk = jnp.concatenate([kb[slot, u, 0], kb[slot, u, 1]], axis=1)
-            vvv = jnp.concatenate([vb[slot, u, 0], vb[slot, u, 1]], axis=1)
-            s = lax.dot_general(q, kk, (((1,), (1,)), ((), ())), preferred_element_type=F32) * (128 ** -0.5)
-            s = jnp.where(tpos <= clen[b], s, -jnp.inf)
-            e = jnp.exp(s - jnp.max(s, axis=-1, keepdims=True))
-            pr = (e / jnp.sum(e, axis=-1, keepdims=True)).astype(BF16)
-            r = jnp.dot(pr, vvv, preferred_element_type=F32)
-            attn[pl.ds(b * 8, 8)] = jnp.where(lo, r[:, :128], r[:, 128:]).astype(BF16).astype(F32)
-
+
+        def weigh(h, carry):
+            for u in range(NB3 // 2):
+                w = h * (NB3 // 2) + u
+                b = i * NB3 + w
+                both = jnp.concatenate([vb[slot, w, 0], vb[slot, w, 1]], axis=1)
+                r = jnp.dot(sscr[w].astype(BF16), both, preferred_element_type=F32)
+                attn[pl.ds(b * 8, 8)] = jnp.where(lo, r[:, :128], r[:, 128:]).astype(BF16).astype(F32)
+            return carry
+
+        lax.fori_loop(0, 2, weigh, 0)
         nxt = i + NS3 - 1
 
         @pl.when(nxt < nstep)
@@ -389,7 +411,7 @@
                    jax.ShapeDtypeStruct((512, 128), F32)),
         in_specs=[ANY, ANY, VMEM, VMEM, VMEM, SMEM],
         out_specs=(ANY, ANY, VMEM),
-        scratch_shapes=[pltpu.VMEM(shape, BF16), pltpu.VMEM(shape, BF16),
+        scratch_shapes=[pltpu.VMEM(shape, BF16), pltpu.VMEM(shape, BF16), pltpu.VMEM((NB3, 8, 512), F32),
                         pltpu.SemaphoreType.DMA((NS3, 2)), pltpu.SemaphoreType.DMA((NS3, 2))],
         compiler_params=pltpu.CompilerParams(vmem_limit_bytes=50 * 2 ** 20),
         name='attention')(kc, vc, qs, kn, vn, clen)

time: 130 us -> 116 us (0.89)
  Pallas kernels: 125 us -> 110 us
    pallas_call x1, Pallas kernels: 30.5 us -> 22.5 us  [k3(): pl.pallas_call(k3_body, out_shape=(jax.ShapeDtypeStruct(kc.shape, BF16),...]
    pallas_call x1, Pallas kernels: 44 us -> 37.7 us  [k1(): pl.pallas_call(k1_body, out_shape=(jax.ShapeDtypeStruct(lin.shape, F32),...]
where the time goes in v2:
time: 116 us
  Pallas kernels  110 us (95%)
  local copies, waits for them, and re-layouts  3.5 us (3%)
    pallas_call x1, Pallas kernels, k1(): pl.pallas_call(k1_body, out_shape=(jax.ShapeDtypeStruct(lin.shape, F32),...  37.7 us
    pallas_call x1, Pallas kernels, k2(): pl.pallas_call(k2_body, out_shape=(jax.ShapeDtypeStruct(h1.shape, BF16),...  29.5 us
    pallas_call x1, Pallas kernels, k3(): pl.pallas_call(k3_body, out_shape=(jax.ShapeDtypeStruct(kc.shape, BF16),...  22.5 us
    pallas_call x1, Pallas kernels, k4(): pl.pallas_call(k4_body, out_shape=jax.ShapeDtypeStruct(h2.shape, BF16), i...  20.7 us
    unnamed x17, local copies, waits for them, and re-layouts  3.32 us

profile of v2, /device:TPU:0, one launch (start us, length us, event | category | flops | bytes accessed | tf_op | source)
XLA Modules:
  0.0 115.7 jit_solution(9269698554229156425)
XLA Ops:
  0.6 0.7 convert_element_type.3
  1.3 0.1 pad.6.clone
  1.4 0.1 pad.3.clone
  1.5 0.2 multiply_sine_fusion
  1.7 0.1 maximum_maximum_fusion
  1.8 0.0 copy-start
  1.8 1.1 copy-done
  2.9 0.0 copy-start.1
  2.9 0.7 copy-done.1
  3.6 0.0 copy-start.6
  3.6 0.7 copy-done.6
  4.3 0.0 copy-start.2
  4.3 0.0 copy-start.3
  4.3 0.0 copy-start.4
  4.3 0.0 copy-start.5
  4.3 37.7 %lightning.1 = (f32[64,8,128,128]{3,2,1,0:T(8,128)}, f32[8,64,128]{2,1,0:T(8,128)S(1)}, f32[8,64,128]{2,1,0:T(8,128)S(1)}, bf16[64,5120]{1,0:T(8,128)(2,1)S(1)}) custom-call(bf16[64,5120]{1,0:T(8,128)(2,1)S(1)} %copy-done, f32[1,5120]{1,0:T(1,128)S(1)} %bitcast.9, bf16[122880,128]{1,0:T(8,128)(2,1)} %bitcast.11, bf16[40960,128]{1,0:T(8,128)(2,1)} %bitcast.13, ...), custom_call_target="tpu_custom_call" | custom-call | tf_op jit(solution)/shard_map/lightning/pallas_call | solution.py:135
  42.0 0.0 copy-start.7
  42.0 0.0 copy-done.2
  42.0 0.0 copy-done.3
  42.0 0.0 copy-done.4
  42.0 0.0 copy-done.5
  42.0 29.5 %mix_first.1 = (bf16[64,5120]{1,0:T(8,128)(2,1)S(1)}, f32[2,512,128]{2,1,0:T(8,128)S(1)}, f32[2,64,128]{2,1,0:T(8,128)S(1)}, f32[2,64,128]{2,1,0:T(8,128)S(1)}) custom-call(f32[8,64,128]{2,1,0:T(8,128)S(1)} %get-tuple-element.15.o_in, f32[8,64,128]{2,1,0:T(8,128)S(1)} %get-tuple-element.16.gate_in, bf16[64,5120]{1,0:T(8,128)(2,1)S(1)} %get-tuple-element.17.h1, ...), custom_call_target="tpu_custom_call" | custom-call | tf_op jit(solution)/shard_map/mix_first/pallas_call | solution.py:306
  71.6 0.0 copy-done.7
  71.6 22.5 %attention.1 = (bf16[64,2,512,128]{3,2,1,0:T(8,128)(2,1)}, bf16[64,2,512,128]{3,2,1,0:T(8,128)(2,1)}, f32[512,128]{1,0:T(8,128)S(1)}) custom-call(bf16[64,2,512,128]{3,2,1,0:T(8,128)(2,1)} %kc.1, bf16[64,2,512,128]{3,2,1,0:T(8,128)(2,1)} %vc.1, f32[2,512,128]{2,1,0:T(8,128)S(1)} %get-tuple-element.18.qs, f32[2,64,128]{2,1,0:T(8,128)S(1)} %get-tuple-element.19.kn, ...), custom_call_target="tpu_custom_call" | custom-call | tf_op jit(solution)/shard_map/attention/pallas_call | solution.py:408
  94.1 20.7 %mix_second.1 = bf16[64,5120]{1,0:T(8,128)(2,1)S(1)} custom-call(f32[512,128]{1,0:T(8,128)S(1)} %get-tuple-element.21.attn, bf16[64,5120]{1,0:T(8,128)(2,1)S(1)} %get-tuple-element.22.h2, bf16[1024,5120]{1,0:T(8,128)(2,1)} %bitcast.15, f32[2]{0:T(128)S(1)} %copy-done.4, f32[2]{0:T(128)S(1)} %copy-done.5), custom_call_target="tpu_custom_call" | custom-call | tf_op jit(solution)/shard_map/mix_second/pallas_call | solution.py:433
  114.8 0.8 copy.21
  (6 shorter events, 0.0 us)
Async XLA Ops:
  1.8 1.1 copy-start
  2.9 0.7 copy-start.1
  3.6 0.7 copy-start.6
  4.3 37.7 %copy-start.2 = (f32[5120]{0:T(1024)S(1)}, f32[5120]{0:T(1024)}, u32[]{:S(2)}) copy-start(f32[5120]{0:T(1024)} %param.27) | copy-start | bytes 61444
  4.3 37.7 %copy-start.3 = (f32[8,128]{1,0:T(8,128)S(1)}, f32[8,128]{1,0:T(8,128)}, u32[]{:S(2)}) copy-start(f32[8,128]{1,0:T(8,128)} %onorm.1) | copy-start | bytes 12292
  4.3 37.8 %copy-start.4 = (f32[2]{0:T(128)S(1)}, f32[2]{0:T(128)}, u32[]{:S(2)}) copy-start(f32[2]{0:T(128)} %alpha.3) | copy-start | bytes 28
  4.3 37.8 %copy-start.5 = (f32[2]{0:T(128)S(1)}, f32[2]{0:T(128)}, u32[]{:S(2)}) copy-start(f32[2]{0:T(128)} %beta.3) | copy-start | bytes 28
  42.0 29.6 %copy-start.7 = (s32[64]{0:T(128)S(1)}, s32[64]{0:T(128)}, u32[]{:S(2)}) copy-start(s32[64]{0:T(128)} %clen.1) | copy-start | bytes 772

commit v3 on v2

--- a/solution.py
+++ b/solution.py
@@ -1,4 +1,4 @@
-import functools
+import math
 import jax
 import jax.numpy as jnp
 from jax import lax
@@ -12,13 +12,14 @@
 BF16 = jnp.bfloat16
 MESH = pl.DeviceIdType.MESH
 ANY = pl.BlockSpec(memory_space=pl.ANY)
+HBM = pl.BlockSpec(memory_space=pltpu.HBM)
 VMEM = pl.BlockSpec(memory_space=pltpu.VMEM)
 SMEM = pl.BlockSpec(memory_space=pltpu.SMEM)
 
 DC = 256
 RS = 9 * DC + 16
 NWB = 4
-NSB = 16
+NSB = 15
 LAG = 4
 
 
@@ -136,7 +137,7 @@
         k1_body,
         out_shape=(jax.ShapeDtypeStruct(lin.shape, F32), jax.ShapeDtypeStruct((8, 64, 128), F32),
                    jax.ShapeDtypeStruct((8, 64, 128), F32), jax.ShapeDtypeStruct(hidden.shape, BF16)),
-        in_specs=[ANY] * 6,
+        in_specs=[HBM] * 6,
         out_specs=(ANY, VMEM, VMEM, VMEM),
         scratch_shapes=[
             pltpu.VMEM((NWB, DC * 24, 128), BF16), pltpu.VMEM((NWB, DC * 8, 128), BF16),
@@ -146,7 +147,8 @@
             pltpu.VMEM(hidden.shape, BF16), pltpu.VMEM(g1.shape, F32), pltpu.SMEM(slopes.shape, F32),
             pltpu.SemaphoreType.DMA((NWB, 2)), pltpu.SemaphoreType.DMA((NSB,)), pltpu.SemaphoreType.DMA((NSB,)),
             pltpu.SemaphoreType.DMA((3,))],
-        compiler_params=pltpu.CompilerParams(vmem_limit_bytes=50 * 2 ** 20),
+        compiler_params=pltpu.CompilerParams(vmem_limit_bytes=34 * 2 ** 20),
+        cost_estimate=pl.CostEstimate(flops=int(5e9), bytes_accessed=int(1.1e8), transcendentals=0),
         name='lightning')(hidden, g1, wqkv, wgate, slopes, lin)
 
 
@@ -171,17 +173,7 @@
     return partner, across, diag
 
 
-def out_weight_copies(w, wo, wosem):
-    core = lax.rem(lax.axis_index('tp'), 2)
-    out = []
-    for s in range(2 * NCH):
-        side = core if s % 2 else 1 - core
-        col = pl.multiple_of(side * HALF + (s // 2) * CW, CW)
-        out.append(pltpu.make_async_copy(w.at[:, pl.ds(col, CW)], wo.at[s], wosem.at[s]))
-    return out
-
-
-def reduce_over_tp(xin, wo, wcopies, full, send_a, recv_a, own, recv_x, sems, between):
+def reduce_over_tp(xin, w, full, send_a, recv_a, own, recv_x, sems, between):
     tp = lax.axis_index('tp')
     core = lax.rem(tp, 2)
     partner, across, _ = peers(tp)
@@ -202,11 +194,11 @@
         cx[j].start()
 
     for j in range(NCH):
-        wcopies[2 * j].wait()
-        send_a[j] = jnp.dot(xin[...], wo[2 * j], preferred_element_type=F32)
+        far = pl.multiple_of((1 - core) * HALF + j * CW, CW)
+        send_a[j] = jnp.dot(xin[...], w[:, pl.ds(far, CW)], preferred_element_type=F32)
         ca[j].start()
-        wcopies[2 * j + 1].wait()
-        own[j] = jnp.dot(xin[...], wo[2 * j + 1], preferred_element_type=F32)
+        near = pl.multiple_of(core * HALF + j * CW, CW)
+        own[j] = jnp.dot(xin[...], w[:, pl.ds(near, CW)], preferred_element_type=F32)
         if j:
             combine(j - 1)
     combine(NCH - 1)
@@ -227,23 +219,21 @@
 REDUCE_SCRATCH = [
     pltpu.VMEM((64, 2 * HALF), F32), pltpu.VMEM((NCH, 64, CW), F32), pltpu.VMEM((NCH, 64, CW), F32),
     pltpu.VMEM((NCH, 64, CW), F32), pltpu.VMEM((NCH, 64, CW), F32),
-    pltpu.VMEM((2 * NCH, 1024, CW), BF16), pltpu.SemaphoreType.DMA((6, NCH)), pltpu.SemaphoreType.DMA((2 * NCH,))]
+    pltpu.SemaphoreType.DMA((6, NCH))]
 
 NAB = 4
-
-
-def k2_body(o_in, gate_in, h1, onorm, w_out, g2, wattn, cosf, sina, sinb, alpha, beta,
+DA = 128
+
+
+def k2_body(o_in, gate_in, h1, onorm, w_out, g2, wattn, clen, alpha, beta,
             h2_out, qs, kn, vn,
-            full, send_a, recv_a, own, recv_x, wo, sems, wosem,
-            xin, ssl, ssr, sssem, abuf, ascr, wd, asem):
+            full, send_a, recv_a, own, recv_x, sems,
+            xin, ssl, ssr, sssem, abuf, ascr, wd, asem, cosf, sina, sinb):
     tp = lax.axis_index('tp')
-    nchunk = h1.shape[1] // DC
-    wcopies = out_weight_copies(w_out, wo, wosem)
-    for c in wcopies:
-        c.start()
+    nchunk = h1.shape[1] // DA
 
     def acopy(i, slot):
-        return pltpu.make_async_copy(wattn.at[pl.ds(i * (DC * 12), DC * 12)], abuf.at[slot], asem.at[slot])
+        return pltpu.make_async_copy(wattn.at[pl.ds(i * (DA * 12), DA * 12)], abuf.at[slot], asem.at[slot])
     for i in range(NAB):
         acopy(i, i).start()
     sq = jnp.zeros((64, 128), F32)
@@ -256,6 +246,18 @@
               for k, dev in enumerate(peers(tp))]
     for c in copies:
         c.start()
+    def spread(b, carry):
+        cosf[pl.ds(b, 1)] = jnp.full((1, 128), clen[b].astype(F32), F32)
+        return carry
+
+    lax.fori_loop(0, 64, spread, 0)
+    lane = lax.broadcasted_iota(jnp.int32, (64, 128), 1)
+    power = (lane & 31).astype(F32) * (-2.0 / 64)
+    angle = cosf[...] * jnp.exp(power * math.log(ROPE_BASE))
+    sine = jnp.sin(angle)
+    cosf[...] = jnp.where(lane < 64, jnp.cos(angle), 1.0)
+    sina[...] = jnp.where(lane < 32, -sine, 0.0)
+    sinb[...] = jnp.where((lane >= 32) & (lane < 64), sine, 0.0)
     for c in copies:
         c.wait_recv()
     total = jnp.sum((ssl[...] + ssr[0]) + (ssr[1] + ssr[2]), axis=-1, keepdims=True)
@@ -269,7 +271,7 @@
         ascr[...] = abuf[slot].astype(F32)
         for j in range(6):
             for kv in range(2):
-                wd[j, kv, pl.ds(pl.multiple_of(i * DC, DC), DC)] = ascr[pl.ds(2 * j + kv, DC, stride=12)].astype(BF16)
+                wd[j, kv, pl.ds(pl.multiple_of(i * DA, DA), DA)] = ascr[pl.ds(2 * j + kv, DA, stride=12)].astype(BF16)
 
         @pl.when(i + NAB < nchunk)
         def _():
@@ -279,7 +281,7 @@
     def between(j):
         lax.fori_loop(j * (nchunk // NCH), (j + 1) * (nchunk // NCH), demix, 0)
 
-    reduce_over_tp(xin, wo, wcopies, full, send_a, recv_a, own, recv_x, sems, between)
+    reduce_over_tp(xin, w_out, full, send_a, recv_a, own, recv_x, sems, between)
     for c in copies:
         c.wait_send()
     mid = (alpha[0] * h1[...].astype(F32) + beta[0] * full[...]).astype(BF16).astype(F32)
@@ -302,20 +304,22 @@
                 vn[kv] = zk.astype(BF16).astype(F32)
 
 
-def k2(o, gate, h1, onorm, w_out, g2, wattn, cosf, sina, sinb, alpha, beta):
+def k2(o, gate, h1, onorm, w_out, g2, wattn, clen, alpha, beta):
     return pl.pallas_call(
         k2_body,
         out_shape=(jax.ShapeDtypeStruct(h1.shape, BF16), jax.ShapeDtypeStruct((2, 512, 128), F32),
                    jax.ShapeDtypeStruct((2, 64, 128), F32), jax.ShapeDtypeStruct((2, 64, 128), F32)),
-        in_specs=[VMEM, VMEM, VMEM, VMEM, ANY, VMEM, ANY, VMEM, VMEM, VMEM, SMEM, SMEM],
+        in_specs=[VMEM, VMEM, VMEM, VMEM, VMEM, VMEM, HBM, SMEM, SMEM, SMEM],
         out_specs=(VMEM, VMEM, VMEM, VMEM),
         scratch_shapes=REDUCE_SCRATCH + [
             pltpu.VMEM((64, 1024), BF16), pltpu.VMEM((64, 128), F32), pltpu.VMEM((3, 64, 128), F32),
             pltpu.SemaphoreType.DMA((2, 3)),
-            pltpu.VMEM((NAB, DC * 12, 128), BF16), pltpu.VMEM((DC * 12, 128), F32),
-            pltpu.VMEM((6, 2, h1.shape[1], 128), BF16), pltpu.SemaphoreType.DMA((NAB,))],
-        compiler_params=pltpu.CompilerParams(vmem_limit_bytes=50 * 2 ** 20, collective_id=0, has_side_effects=True),
-        name='mix_first')(o, gate, h1, onorm, w_out, g2, wattn, cosf, sina, sinb, alpha, beta)
+            pltpu.VMEM((NAB, DA * 12, 128), BF16), pltpu.VMEM((DA * 12, 128), F32),
+            pltpu.VMEM((6, 2, h1.shape[1], 128), BF16), pltpu.SemaphoreType.DMA((NAB,)),
+            pltpu.VMEM((64, 128), F32), pltpu.VMEM((64, 128), F32), pltpu.VMEM((64, 128), F32)],
+        compiler_params=pltpu.CompilerParams(vmem_limit_bytes=24 * 2 ** 20, collective_id=0, has_side_effects=True),
+        cost_estimate=pl.CostEstimate(flops=int(6e10), bytes_accessed=int(2e7), transcendentals=0),
+        name='mix_first')(o, gate, h1, onorm, w_out, g2, wattn, clen, alpha, beta)
 
 
 NB3 = 8
@@ -326,8 +330,7 @@
     nstep = kc.shape[0] // NB3
 
     def reads(i, slot):
-        return (pltpu.make_async_copy(kc.at[pl.ds(i * NB3, NB3)], kb.at[slot], rsem.at[slot, 0]),
-                pltpu.make_async_copy(vc.at[pl.ds(i * NB3, NB3)], vb.at[slot], rsem.at[slot, 1]))
+        return (pltpu.make_async_copy(vc.at[pl.ds(i * NB3, NB3)], vb.at[slot], rsem.at[slot, 1]),)
 
     def writes(i, slot):
         return (pltpu.make_async_copy(kb.at[slot], k_out.at[pl.ds(i * NB3, NB3)], wsem.at[slot, 0]),
@@ -341,6 +344,7 @@
         slot = lax.rem(i, NS3)
         for c in reads(i, slot):
             c.wait()
+        kb[slot] = kc[pl.ds(i * NB3, NB3)]
         row_id = lax.broadcasted_iota(jnp.int32, (16, 128), 0)
         for u in range(NB3):
             b = i * NB3 + u
@@ -409,23 +413,21 @@
         k3_body,
         out_shape=(jax.ShapeDtypeStruct(kc.shape, BF16), jax.ShapeDtypeStruct(vc.shape, BF16),
                    jax.ShapeDtypeStruct((512, 128), F32)),
-        in_specs=[ANY, ANY, VMEM, VMEM, VMEM, SMEM],
+        in_specs=[VMEM, HBM, VMEM, VMEM, VMEM, SMEM],
         out_specs=(ANY, ANY, VMEM),
         scratch_shapes=[pltpu.VMEM(shape, BF16), pltpu.VMEM(shape, BF16), pltpu.VMEM((NB3, 8, 512), F32),
                         pltpu.SemaphoreType.DMA((NS3, 2)), pltpu.SemaphoreType.DMA((NS3, 2))],
-        compiler_params=pltpu.CompilerParams(vmem_limit_bytes=50 * 2 ** 20),
+        compiler_params=pltpu.CompilerParams(vmem_limit_bytes=20 * 2 ** 20),
+        cost_estimate=pl.CostEstimate(flops=int(1e9), bytes_accessed=int(6e7), transcendentals=0),
         name='attention')(kc, vc, qs, kn, vn, clen)
 
 
 def k4_body(attn, h2, w_out, alpha, beta, out,
-            full, send_a, recv_a, own, recv_x, wo, sems, wosem, xin):
-    wcopies = out_weight_copies(w_out, wo, wosem)
-    for c in wcopies:
-        c.start()
+            full, send_a, recv_a, own, recv_x, sems, xin):
     for r in range(8):
         xin[:, r * 128:(r + 1) * 128] = attn[pl.ds(r, 64, stride=8)].astype(BF16)
     entry_barrier()
-    reduce_over_tp(xin, wo, wcopies, full, send_a, recv_a, own, recv_x, sems, lambda j: None)
+    reduce_over_tp(xin, w_out, full, send_a, recv_a, own, recv_x, sems, lambda j: None)
     out[...] = (alpha[1] * h2[...].astype(F32) + beta[1] * full[...]).astype(BF16)
 
 
@@ -433,23 +435,12 @@
     return pl.pallas_call(
         k4_body,
         out_shape=jax.ShapeDtypeStruct(h2.shape, BF16),
-        in_specs=[VMEM, VMEM, ANY, SMEM, SMEM],
+        in_specs=[VMEM, VMEM, VMEM, SMEM, SMEM],
         out_specs=VMEM,
         scratch_shapes=REDUCE_SCRATCH + [pltpu.VMEM((64, 1024), BF16)],
-        compiler_params=pltpu.CompilerParams(vmem_limit_bytes=50 * 2 ** 20, collective_id=1, has_side_effects=True),
+        compiler_params=pltpu.CompilerParams(vmem_limit_bytes=11 * 2 ** 20, collective_id=1, has_side_effects=True),
+        cost_estimate=pl.CostEstimate(flops=int(2e10), bytes_accessed=int(2e6), transcendentals=0),
         name='mix_second')(attn, h2, w_out, alpha, beta)
-
-
-def rope_tables(clen):
-    inv_freq = ROPE_BASE ** (-2.0 * jnp.arange(32, dtype=F32) / 64)
-    ang = clen.astype(F32)[:, None] * inv_freq[None, :]
-    cos, sin = jnp.cos(ang), jnp.sin(ang)
-    zero = jnp.zeros((clen.shape[0], 32), F32)
-    one = jnp.ones((clen.shape[0], 64), F32)
-    cosf = jnp.concatenate([cos, cos, one], axis=1)
-    sina = jnp.concatenate([-sin, zero, zero, zero], axis=1)
-    sinb = jnp.concatenate([zero, sin, zero, zero], axis=1)
-    return cosf, sina, sinb
 
 
 def solution(mesh):
@@ -463,13 +454,15 @@
     def local_step(hidden, cache_len, lin_state, k_cache, v_cache, norm_first, w_qkv, w_gate, slopes, out_norm,
                    w_out_lin, norm_second, w_attn, w_out_attn, mix_alpha, mix_beta):
         d = hidden.shape[1]
-        cosf, sina, sinb = rope_tables(cache_len)
-        state_out, o, gate, h1 = k1(hidden, norm_first.reshape(1, d), w_qkv.reshape(-1, 128),
-                                    w_gate.reshape(-1, 128), slopes, lin_state)
-        wattn = jnp.transpose(w_attn, (0, 2, 1, 3)).reshape(-1, 128)
+
+        def pin(x):
+            return pltpu.with_memory_space_constraint(x, pltpu.HBM)
+        state_out, o, gate, h1 = k1(pin(hidden), pin(norm_first.reshape(1, d)), pin(w_qkv.reshape(-1, 128)),
+                                    pin(w_gate.reshape(-1, 128)), pin(slopes), pin(lin_state))
+        wattn = pin(jnp.transpose(w_attn, (0, 2, 1, 3)).reshape(-1, 128))
         h2, qs, kn, vn = k2(o, gate, h1, out_norm, w_out_lin.reshape(-1, d), norm_second.reshape(1, d), wattn,
-                            cosf, sina, sinb, mix_alpha, mix_beta)
-        k_out, v_out, attn = k3(k_cache, v_cache, qs, kn, vn, cache_len)
+                            cache_len, mix_alpha, mix_beta)
+        k_out, v_out, attn = k3(k_cache, pin(v_cache), qs, kn, vn, cache_len)
         hidden_out = k4(attn, h2, w_out_attn.reshape(-1, d), mix_alpha, mix_beta)
         return hidden_out, state_out, k_out, v_out
 

time: 116 us -> 114 us (0.983)
  local copies, waits for them, and re-layouts: 3.5 us -> 0.9 us
  Pallas kernels: 110 us -> 112 us
    pallas_call x1, Pallas kernels: 37.7 us -> 40.7 us  [k1(): pl.pallas_call(k1_body, out_shape=(jax.ShapeDtypeStruct(lin.shape, F32),...]
    unnamed x17 -> x23, local copies, waits for them, and re-layouts: 3.32 us -> 0.9 us
    pallas_call x1, Pallas kernels: 22.5 us -> 20.8 us  [k3(): pl.pallas_call(k3_body, out_shape=(jax.ShapeDtypeStruct(kc.shape, BF16),...]
where the time goes in v3:
time: 114 us; the launch traced here: 113 us
  Pallas kernels  112 us (98%)
    pallas_call x1, Pallas kernels, k1(): pl.pallas_call(k1_body, out_shape=(jax.ShapeDtypeStruct(lin.shape, F32),...  40.7 us
    pallas_call x1, Pallas kernels, k2(): pl.pallas_call(k2_body, out_shape=(jax.ShapeDtypeStruct(h1.shape, BF16),...  29.4 us
    pallas_call x1, Pallas kernels, k3(): pl.pallas_call(k3_body, out_shape=(jax.ShapeDtypeStruct(kc.shape, BF16),...  20.8 us
    pallas_call x1, Pallas kernels, k4(): pl.pallas_call(k4_body, out_shape=jax.ShapeDtypeStruct(h2.shape, BF16), i...  20.7 us

profile of v3, /device:TPU:0, one launch (start us, length us, event | category | flops | bytes accessed | tf_op | source)
XLA Modules:
  0.0 113.3 jit_solution(12109732215407424217)
XLA Ops:
  0.6 0.0 copy-start
  0.6 0.0 copy-start.1
  0.7 0.0 copy-start.3
  0.7 0.0 copy-start.4
  0.7 0.0 copy-start.5
  0.7 0.0 copy-start.6
  0.7 0.0 slice-start
  0.7 0.0 slice-start.1
  0.7 40.7 %lightning.1 = (f32[64,8,128,128]{3,2,1,0:T(8,128)}, f32[8,64,128]{2,1,0:T(8,128)S(1)}, f32[8,64,128]{2,1,0:T(8,128)S(1)}, bf16[64,5120]{1,0:T(8,128)(2,1)S(1)}) custom-call(bf16[64,5120]{1,0:T(8,128)(2,1)} %hid_hbm.1, f32[1,5120]{1,0:T(1,128)} %bitcast.16, bf16[122880,128]{1,0:T(8,128)(2,1)} %bitcast.14, bf16[40960,128]{1,0:T(8,128)(2,1)} %bitcast.15, ...), custom_call_target="tpu_custom_call" | custom-call | flops 5000000000 | bytes 110000000 | tf_op jit(solution)/shard_map/lightning/pallas_call | solution.py:136
  41.4 0.0 copy-done
  41.4 0.0 copy-done.1
  41.4 0.0 copy-done.3
  41.4 0.0 copy-done.4
  41.4 0.0 copy-done.5
  41.5 0.0 copy-done.6
  41.5 0.0 slice-start.2
  41.5 0.0 slice-start.3
  41.5 29.4 %mix_first.1 = (bf16[64,5120]{1,0:T(8,128)(2,1)S(1)}, f32[2,512,128]{2,1,0:T(8,128)S(1)}, f32[2,64,128]{2,1,0:T(8,128)S(1)}, f32[2,64,128]{2,1,0:T(8,128)S(1)}) custom-call(f32[8,64,128]{2,1,0:T(8,128)S(1)} %get-tuple-element.15.o_in, f32[8,64,128]{2,1,0:T(8,128)S(1)} %get-tuple-element.16.gate_in, bf16[64,5120]{1,0:T(8,128)(2,1)S(1)} %get-tuple-element.17.h1, ...), custom_call_target="tpu_custom_call" | custom-call | flops 60000002048 | bytes 20000000 | tf_op jit(solution)/shard_map/mix_first/pallas_call | solution.py:308
  70.9 0.0 slice-done
  70.9 0.0 slice-done.1
  70.9 0.0 slice-done.2
  70.9 0.0 slice-done.3
  70.9 0.0 copy-start.2
  70.9 20.8 %attention.1 = (bf16[64,2,512,128]{3,2,1,0:T(8,128)(2,1)}, bf16[64,2,512,128]{3,2,1,0:T(8,128)(2,1)}, f32[512,128]{1,0:T(8,128)S(1)}) custom-call(bf16[64,2,512,128]{3,2,1,0:T(8,128)(2,1)S(1)} %bitcast.10, bf16[64,2,512,128]{3,2,1,0:T(8,128)(2,1)} %vc.1, f32[2,512,128]{2,1,0:T(8,128)S(1)} %get-tuple-element.18.qs, f32[2,64,128]{2,1,0:T(8,128)S(1)} %get-tuple-element.19.kn, ...), custom_call_target="tpu_custom_call" | custom-call | flops 1000000000 | bytes 60000000 | tf_op jit(solution)/shard_map/attention/pallas_call | solution.py:412
  91.7 0.0 copy-done.2
  91.7 20.7 %mix_second.1 = bf16[64,5120]{1,0:T(8,128)(2,1)S(1)} custom-call(f32[512,128]{1,0:T(8,128)S(1)} %get-tuple-element.21.attn, bf16[64,5120]{1,0:T(8,128)(2,1)S(1)} %get-tuple-element.22.h2, bf16[1024,5120]{1,0:T(8,128)(2,1)S(1)} %bitcast.12, f32[2]{0:T(128)S(1)} %copy-done.5, f32[2]{0:T(128)S(1)} %copy-done.6), custom_call_target="tpu_custom_call" | custom-call | flops 20000000000 | bytes 2000000 | tf_op jit(solution)/shard_map/mix_second/pallas_call | solution.py:435
  112.4 0.8 copy.21
  (1 shorter events, 0.0 us)
Async XLA Ops:
  0.6 40.8 %copy-start = (s32[64]{0:T(128)S(1)}, s32[64]{0:T(128)}, u32[]{:S(2)}) copy-start(s32[64]{0:T(128)} %clen.3) | copy-start | bytes 772
  0.6 40.8 %copy-start.1 = (bf16[8,128,5120]{2,1,0:T(8,128)(2,1)S(1)}, bf16[8,128,5120]{2,1,0:T(8,128)(2,1)}, u32[]{:S(2)}) copy-start(bf16[8,128,5120]{2,1,0:T(8,128)(2,1)} %param.26) | copy-start | bytes 31457284
  0.7 40.8 %copy-start.3 = (f32[5120]{0:T(1024)S(1)}, f32[5120]{0:T(1024)}, u32[]{:S(2)}) copy-start(f32[5120]{0:T(1024)} %param.27) | copy-start | bytes 61444
  0.7 40.8 %copy-start.4 = (f32[8,128]{1,0:T(8,128)S(1)}, f32[8,128]{1,0:T(8,128)}, u32[]{:S(2)}) copy-start(f32[8,128]{1,0:T(8,128)} %onorm.1) | copy-start | bytes 12292
  0.7 40.8 %copy-start.5 = (f32[2]{0:T(128)S(1)}, f32[2]{0:T(128)}, u32[]{:S(2)}) copy-start(f32[2]{0:T(128)} %alpha.3) | copy-start | bytes 28
  0.7 40.8 %copy-start.6 = (f32[2]{0:T(128)S(1)}, f32[2]{0:T(128)}, u32[]{:S(2)}) copy-start(f32[2]{0:T(128)} %beta.3) | copy-start | bytes 28
  0.7 70.2 %slice-start = ((s8[16777216]{0:T(1024)(128)(4,1)}), s8[4194304]{0:T(1024)(128)(4,1)S(1)}, s32[]{:S(2)}) async-start(s8[16777216]{0:T(1024)(128)(4,1)} %bitcast.9), calls=%async_computation | async-start | bytes 8388608
  0.7 70.2 %slice-start.1 = ((s8[16777216]{0:T(1024)(128)(4,1)}), s8[4194304]{0:T(1024)(128)(4,1)S(1)}, s32[]{:S(2)}) async-start(s8[16777216]{0:T(1024)(128)(4,1)} %bitcast.9), calls=%async_computation.1 | async-start | bytes 8388608
  41.5 29.4 %slice-start.2 = ((s8[16777216]{0:T(1024)(128)(4,1)}), s8[4194304]{0:T(1024)(128)(4,1)S(1)}, s32[]{:S(2)}) async-start(s8[16777216]{0:T(1024)(128)(4,1)} %bitcast.9), calls=%async_computation.2 | async-start | bytes 8388608
  41.5 29.4 %slice-start.3 = ((s8[16777216]{0:T(1024)(128)(4,1)}), s8[4194304]{0:T(1024)(128)(4,1)S(1)}, s32[]{:S(2)}) async-start(s8[16777216]{0:T(1024)(128)(4,1)} %bitcast.9), calls=%async_computation.3 | async-start | bytes 8388608
  70.9 20.8 %copy-start.2 = (bf16[8,128,5120]{2,1,0:T(8,128)(2,1)S(1)}, bf16[8,128,5120]{2,1,0:T(8,128)(2,1)}, u32[]{:S(2)}) copy-start(bf16[8,128,5120]{2,1,0:T(8,128)(2,1)} %param.29) | copy-start | bytes 31457284

commit v4 on v3

--- a/solution.py
+++ b/solution.py
@@ -148,7 +148,7 @@
             pltpu.SemaphoreType.DMA((NWB, 2)), pltpu.SemaphoreType.DMA((NSB,)), pltpu.SemaphoreType.DMA((NSB,)),
             pltpu.SemaphoreType.DMA((3,))],
         compiler_params=pltpu.CompilerParams(vmem_limit_bytes=34 * 2 ** 20),
-        cost_estimate=pl.CostEstimate(flops=int(5e9), bytes_accessed=int(1.1e8), transcendentals=0),
+        cost_estimate=pl.CostEstimate(flops=int(1e12), bytes_accessed=int(1.1e8), transcendentals=0),
         name='lightning')(hidden, g1, wqkv, wgate, slopes, lin)
 
 
@@ -173,7 +173,17 @@
     return partner, across, diag
 
 
-def reduce_over_tp(xin, w, full, send_a, recv_a, own, recv_x, sems, between):
+def out_weight_copies(w, wo, wosem):
+    core = lax.rem(lax.axis_index('tp'), 2)
+    out = []
+    for s in range(2 * NCH):
+        side = core if s % 2 else 1 - core
+        col = pl.multiple_of(side * HALF + (s // 2) * CW, CW)
+        out.append(pltpu.make_async_copy(w.at[:, pl.ds(col, CW)], wo.at[s], wosem.at[s]))
+    return out
+
+
+def reduce_over_tp(xin, wo, wcopies, full, send_a, recv_a, own, recv_x, sems, between):
     tp = lax.axis_index('tp')
     core = lax.rem(tp, 2)
     partner, across, _ = peers(tp)
@@ -194,11 +204,11 @@
         cx[j].start()
 
     for j in range(NCH):
-        far = pl.multiple_of((1 - core) * HALF + j * CW, CW)
-        send_a[j] = jnp.dot(xin[...], w[:, pl.ds(far, CW)], preferred_element_type=F32)
+        wcopies[2 * j].wait()
+        send_a[j] = jnp.dot(xin[...], wo[2 * j], preferred_element_type=F32)
         ca[j].start()
-        near = pl.multiple_of(core * HALF + j * CW, CW)
-        own[j] = jnp.dot(xin[...], w[:, pl.ds(near, CW)], preferred_element_type=F32)
+        wcopies[2 * j + 1].wait()
+        own[j] = jnp.dot(xin[...], wo[2 * j + 1], preferred_element_type=F32)
         if j:
             combine(j - 1)
     combine(NCH - 1)
@@ -219,18 +229,21 @@
 REDUCE_SCRATCH = [
     pltpu.VMEM((64, 2 * HALF), F32), pltpu.VMEM((NCH, 64, CW), F32), pltpu.VMEM((NCH, 64, CW), F32),
     pltpu.VMEM((NCH, 64, CW), F32), pltpu.VMEM((NCH, 64, CW), F32),
-    pltpu.SemaphoreType.DMA((6, NCH))]
-
-NAB = 4
+    pltpu.VMEM((2 * NCH, 1024, CW), BF16), pltpu.SemaphoreType.DMA((6, NCH)), pltpu.SemaphoreType.DMA((2 * NCH,))]
+
+NAB = 8
 DA = 128
 
 
 def k2_body(o_in, gate_in, h1, onorm, w_out, g2, wattn, clen, alpha, beta,
             h2_out, qs, kn, vn,
-            full, send_a, recv_a, own, recv_x, sems,
+            full, send_a, recv_a, own, recv_x, wo, sems, wosem,
             xin, ssl, ssr, sssem, abuf, ascr, wd, asem, cosf, sina, sinb):
     tp = lax.axis_index('tp')
     nchunk = h1.shape[1] // DA
+    wcopies = out_weight_copies(w_out, wo, wosem)
+    for c in wcopies:
+        c.start()
 
     def acopy(i, slot):
         return pltpu.make_async_copy(wattn.at[pl.ds(i * (DA * 12), DA * 12)], abuf.at[slot], asem.at[slot])
@@ -281,7 +294,7 @@
     def between(j):
         lax.fori_loop(j * (nchunk // NCH), (j + 1) * (nchunk // NCH), demix, 0)
 
-    reduce_over_tp(xin, w_out, full, send_a, recv_a, own, recv_x, sems, between)
+    reduce_over_tp(xin, wo, wcopies, full, send_a, recv_a, own, recv_x, sems, between)
     for c in copies:
         c.wait_send()
     mid = (alpha[0] * h1[...].astype(F32) + beta[0] * full[...]).astype(BF16).astype(F32)
@@ -309,7 +322,7 @@
         k2_body,
         out_shape=(jax.ShapeDtypeStruct(h1.shape, BF16), jax.ShapeDtypeStruct((2, 512, 128), F32),
                    jax.ShapeDtypeStruct((2, 64, 128), F32), jax.ShapeDtypeStruct((2, 64, 128), F32)),
-        in_specs=[VMEM, VMEM, VMEM, VMEM, VMEM, VMEM, HBM, SMEM, SMEM, SMEM],
+        in_specs=[VMEM, VMEM, VMEM, VMEM, HBM, VMEM, HBM, SMEM, SMEM, SMEM],
         out_specs=(VMEM, VMEM, VMEM, VMEM),
         scratch_shapes=REDUCE_SCRATCH + [
             pltpu.VMEM((64, 1024), BF16), pltpu.VMEM((64, 128), F32), pltpu.VMEM((3, 64, 128), F32),
@@ -317,7 +330,7 @@
             pltpu.VMEM((NAB, DA * 12, 128), BF16), pltpu.VMEM((DA * 12, 128), F32),
             pltpu.VMEM((6, 2, h1.shape[1], 128), BF16), pltpu.SemaphoreType.DMA((NAB,)),
             pltpu.VMEM((64, 128), F32), pltpu.VMEM((64, 128), F32), pltpu.VMEM((64, 128), F32)],
-        compiler_params=pltpu.CompilerParams(vmem_limit_bytes=24 * 2 ** 20, collective_id=0, has_side_effects=True),
+        compiler_params=pltpu.CompilerParams(vmem_limit_bytes=36 * 2 ** 20, collective_id=0, has_side_effects=True),
         cost_estimate=pl.CostEstimate(flops=int(6e10), bytes_accessed=int(2e7), transcendentals=0),
         name='mix_first')(o, gate, h1, onorm, w_out, g2, wattn, clen, alpha, beta)
 
@@ -423,11 +436,14 @@
 
 
 def k4_body(attn, h2, w_out, alpha, beta, out,
-            full, send_a, recv_a, own, recv_x, sems, xin):
+            full, send_a, recv_a, own, recv_x, wo, sems, wosem, xin):
+    wcopies = out_weight_copies(w_out, wo, wosem)
+    for c in wcopies:
+        c.start()
     for r in range(8):
         xin[:, r * 128:(r + 1) * 128] = attn[pl.ds(r, 64, stride=8)].astype(BF16)
     entry_barrier()
-    reduce_over_tp(xin, w_out, full, send_a, recv_a, own, recv_x, sems, lambda j: None)
+    reduce_over_tp(xin, wo, wcopies, full, send_a, recv_a, own, recv_x, sems, lambda j: None)
     out[...] = (alpha[1] * h2[...].astype(F32) + beta[1] * full[...]).astype(BF16)
 
 
@@ -435,10 +451,10 @@
     return pl.pallas_call(
         k4_body,
         out_shape=jax.ShapeDtypeStruct(h2.shape, BF16),
-        in_specs=[VMEM, VMEM, VMEM, SMEM, SMEM],
+        in_specs=[VMEM, VMEM, HBM, SMEM, SMEM],
         out_specs=VMEM,
         scratch_shapes=REDUCE_SCRATCH + [pltpu.VMEM((64, 1024), BF16)],
-        compiler_params=pltpu.CompilerParams(vmem_limit_bytes=11 * 2 ** 20, collective_id=1, has_side_effects=True),
+        compiler_params=pltpu.CompilerParams(vmem_limit_bytes=20 * 2 ** 20, collective_id=1, has_side_effects=True),
         cost_estimate=pl.CostEstimate(flops=int(2e10), bytes_accessed=int(2e6), transcendentals=0),
         name='mix_second')(attn, h2, w_out, alpha, beta)
 
@@ -460,10 +476,10 @@
         state_out, o, gate, h1 = k1(pin(hidden), pin(norm_first.reshape(1, d)), pin(w_qkv.reshape(-1, 128)),
                                     pin(w_gate.reshape(-1, 128)), pin(slopes), pin(lin_state))
         wattn = pin(jnp.transpose(w_attn, (0, 2, 1, 3)).reshape(-1, 128))
-        h2, qs, kn, vn = k2(o, gate, h1, out_norm, w_out_lin.reshape(-1, d), norm_second.reshape(1, d), wattn,
+        h2, qs, kn, vn = k2(o, gate, h1, out_norm, pin(w_out_lin.reshape(-1, d)), norm_second.reshape(1, d), wattn,
                             cache_len, mix_alpha, mix_beta)
         k_out, v_out, attn = k3(k_cache, pin(v_cache), qs, kn, vn, cache_len)
-        hidden_out = k4(attn, h2, w_out_attn.reshape(-1, d), mix_alpha, mix_beta)
+        hidden_out = k4(attn, h2, pin(w_out_attn.reshape(-1, d)), mix_alpha, mix_beta)
         return hidden_out, state_out, k_out, v_out
 
     return jax.shard_map(local_step, mesh=mesh, in_specs=in_specs, out_specs=out_specs, check_vma=False)

time: 114 us -> 108 us (0.947)
  Pallas kernels: 112 us -> 107 us
    pallas_call x1, Pallas kernels: 20.8 us -> 17.2 us  [k3(): pl.pallas_call(k3_body, out_shape=(jax.ShapeDtypeStruct(kc.shape, BF16),...]
    pallas_call x1, Pallas kernels: 40.7 us -> 39 us  [k1(): pl.pallas_call(k1_body, out_shape=(jax.ShapeDtypeStruct(lin.shape, F32),...]
where the time goes in v4:
time: 108 us
  Pallas kernels  107 us (99%)
    pallas_call x1, Pallas kernels, k1(): pl.pallas_call(k1_body, out_shape=(jax.ShapeDtypeStruct(lin.shape, F32),...  39 us
    pallas_call x1, Pallas kernels, k2(): pl.pallas_call(k2_body, out_shape=(jax.ShapeDtypeStruct(h1.shape, BF16),...  29.7 us
    pallas_call x1, Pallas kernels, k4(): pl.pallas_call(k4_body, out_shape=jax.ShapeDtypeStruct(h2.shape, BF16), i...  20.8 us
    pallas_call x1, Pallas kernels, k3(): pl.pallas_call(k3_body, out_shape=(jax.ShapeDtypeStruct(kc.shape, BF16),...  17.2 us

profile of v4, /device:TPU:0, one launch (start us, length us, event | category | flops | bytes accessed | tf_op | source)
XLA Modules:
  0.0 108.3 jit_solution(5418632805351506730)
XLA Ops:
  0.6 0.0 copy-start.1
  0.6 0.0 copy-start.2
  0.7 0.0 copy-start.3
  0.7 0.0 copy-start.4
  0.7 0.0 copy-start.5
  0.7 39.0 %lightning.1 = (f32[64,8,128,128]{3,2,1,0:T(8,128)}, f32[8,64,128]{2,1,0:T(8,128)S(1)}, f32[8,64,128]{2,1,0:T(8,128)S(1)}, bf16[64,5120]{1,0:T(8,128)(2,1)S(1)}) custom-call(bf16[64,5120]{1,0:T(8,128)(2,1)} %hid_hbm.1, f32[1,5120]{1,0:T(1,128)} %bitcast.15, bf16[122880,128]{1,0:T(8,128)(2,1)} %bitcast.10, bf16[40960,128]{1,0:T(8,128)(2,1)} %bitcast.12, ...), custom_call_target="tpu_custom_call" | custom-call | flops 999999995904 | bytes 110000000 | tf_op jit(solution)/shard_map/lightning/pallas_call | solution.py:136
  39.7 0.0 copy-done.1
  39.7 0.0 copy-done.2
  39.7 0.0 copy-done.3
  39.7 0.0 copy-done.4
  39.7 0.0 copy-done.5
  39.8 0.0 copy-start
  39.8 29.7 %mix_first.1 = (bf16[64,5120]{1,0:T(8,128)(2,1)S(1)}, f32[2,512,128]{2,1,0:T(8,128)S(1)}, f32[2,64,128]{2,1,0:T(8,128)S(1)}, f32[2,64,128]{2,1,0:T(8,128)S(1)}) custom-call(f32[8,64,128]{2,1,0:T(8,128)S(1)} %get-tuple-element.15.o_in, f32[8,64,128]{2,1,0:T(8,128)S(1)} %get-tuple-element.16.gate_in, bf16[64,5120]{1,0:T(8,128)(2,1)S(1)} %get-tuple-element.17.h1, ...), custom_call_target="tpu_custom_call" | custom-call | flops 60000002048 | bytes 20000000 | tf_op jit(solution)/shard_map/mix_first/pallas_call | solution.py:321
  69.5 0.0 copy-done
  69.5 17.2 %attention.1 = (bf16[64,2,512,128]{3,2,1,0:T(8,128)(2,1)}, bf16[64,2,512,128]{3,2,1,0:T(8,128)(2,1)}, f32[512,128]{1,0:T(8,128)S(1)}) custom-call(bf16[64,2,512,128]{3,2,1,0:T(8,128)(2,1)S(1)} %copy-done, bf16[64,2,512,128]{3,2,1,0:T(8,128)(2,1)} %vc.1, f32[2,512,128]{2,1,0:T(8,128)S(1)} %get-tuple-element.18.qs, f32[2,64,128]{2,1,0:T(8,128)S(1)} %get-tuple-element.19.kn, ...), custom_call_target="tpu_custom_call" | custom-call | flops 1000000000 | bytes 60000000 | tf_op jit(solution)/shard_map/attention/pallas_call | solution.py:425
  86.7 20.8 %mix_second.1 = bf16[64,5120]{1,0:T(8,128)(2,1)S(1)} custom-call(f32[512,128]{1,0:T(8,128)S(1)} %get-tuple-element.21.attn, bf16[64,5120]{1,0:T(8,128)(2,1)S(1)} %get-tuple-element.22.h2, bf16[1024,5120]{1,0:T(8,128)(2,1)} %bitcast.14, f32[2]{0:T(128)S(1)} %copy-done.4, f32[2]{0:T(128)S(1)} %copy-done.5), custom_call_target="tpu_custom_call" | custom-call | flops 20000000000 | bytes 2000000 | tf_op jit(solution)/shard_map/mix_second/pallas_call | solution.py:451
  107.5 0.8 copy.21
Async XLA Ops:
  0.6 39.1 %copy-start.1 = (s32[64]{0:T(128)S(1)}, s32[64]{0:T(128)}, u32[]{:S(2)}) copy-start(s32[64]{0:T(128)} %clen.3) | copy-start | bytes 772
  0.6 39.1 %copy-start.2 = (f32[5120]{0:T(1024)S(1)}, f32[5120]{0:T(1024)}, u32[]{:S(2)}) copy-start(f32[5120]{0:T(1024)} %param.27) | copy-start | bytes 61444
  0.7 39.1 %copy-start.3 = (f32[8,128]{1,0:T(8,128)S(1)}, f32[8,128]{1,0:T(8,128)}, u32[]{:S(2)}) copy-start(f32[8,128]{1,0:T(8,128)} %onorm.1) | copy-start | bytes 12292
  0.7 39.1 %copy-start.4 = (f32[2]{0:T(128)S(1)}, f32[2]{0:T(128)}, u32[]{:S(2)}) copy-start(f32[2]{0:T(128)} %alpha.3) | copy-start | bytes 28
  0.7 39.1 %copy-start.5 = (f32[2]{0:T(128)S(1)}, f32[2]{0:T(128)}, u32[]{:S(2)}) copy-start(f32[2]{0:T(128)} %beta.3) | copy-start | bytes 28
  39.8 29.8 %copy-start = (bf16[64,2,512,128]{3,2,1,0:T(8,128)(2,1)S(1)}, bf16[64,2,512,128]{3,2,1,0:T(8,128)(2,1)}, u32[]{:S(2)}) copy-start(bf16[64,2,512,128]{3,2,1,0:T(8,128)(2,1)} %kc.1) | copy-start | bytes 50331652

commit v5 on v4

--- a/solution.py
+++ b/solution.py
@@ -18,9 +18,10 @@
 
 DC = 256
 RS = 9 * DC + 16
-NWB = 4
-NSB = 15
-LAG = 4
+NWB = 5
+NSB = 23
+LAG = 2
+LATE = 17
 
 
 def k1_body(hid_hbm, g1_hbm, wqkv, wgate, slopes_hbm, lin, st_out, o_out, gate_out, h1_out,
@@ -77,9 +78,11 @@
             for c in wcopies(i + NWB, slot):
                 c.start()
 
-        @pl.when(i < NSB)
-        def _():
-            sread(i, i).start()
+        sread(i, i).start()
+
+        @pl.when(i >= LATE)
+        def _():
+            sread(i - LATE + nchunk, i - LATE + nchunk).start()
         return carry
 
     lax.fori_loop(0, nchunk, wstep, 0)
@@ -147,10 +150,14 @@
             pltpu.VMEM(hidden.shape, BF16), pltpu.VMEM(g1.shape, F32), pltpu.SMEM(slopes.shape, F32),
             pltpu.SemaphoreType.DMA((NWB, 2)), pltpu.SemaphoreType.DMA((NSB,)), pltpu.SemaphoreType.DMA((NSB,)),
             pltpu.SemaphoreType.DMA((3,))],
-        compiler_params=pltpu.CompilerParams(vmem_limit_bytes=34 * 2 ** 20),
+        compiler_params=pltpu.CompilerParams(vmem_limit_bytes=45 * 2 ** 20),
         cost_estimate=pl.CostEstimate(flops=int(1e12), bytes_accessed=int(1.1e8), transcendentals=0),
         name='lightning')(hidden, g1, wqkv, wgate, slopes, lin)
 
+
+NB3 = 8
+NS3 = 4
+NPRE = 3
 
 NCH = 5
 CW = 512
@@ -179,7 +186,8 @@
     for s in range(2 * NCH):
         side = core if s % 2 else 1 - core
         col = pl.multiple_of(side * HALF + (s // 2) * CW, CW)
-        out.append(pltpu.make_async_copy(w.at[:, pl.ds(col, CW)], wo.at[s], wosem.at[s]))
+        slot = s % wo.shape[0]
+        out.append(pltpu.make_async_copy(w.at[:, pl.ds(col, CW)], wo.at[slot], wosem.at[slot]))
     return out
 
 
@@ -198,17 +206,22 @@
         col = pl.multiple_of(core * HALF + j * CW, CW)
         cf.append(rcopy(full.at[:, pl.ds(col, CW)], full.at[:, pl.ds(col, CW)], 4, j, partner))
 
+    def product(n):
+        wcopies[n].wait()
+        out = jnp.dot(xin[...], wo[n % wo.shape[0]], preferred_element_type=F32)
+        if n + wo.shape[0] < 2 * NCH:
+            wcopies[n + wo.shape[0]].start()
+        return out
+
     def combine(j):
         ca[j].wait_recv()
         own[j] = own[j] + recv_a[j]
         cx[j].start()
 
     for j in range(NCH):
-        wcopies[2 * j].wait()
-        send_a[j] = jnp.dot(xin[...], wo[2 * j], preferred_element_type=F32)
+        send_a[j] = product(2 * j)
         ca[j].start()
-        wcopies[2 * j + 1].wait()
-        own[j] = jnp.dot(xin[...], wo[2 * j + 1], preferred_element_type=F32)
+        own[j] = product(2 * j + 1)
         if j:
             combine(j - 1)
     combine(NCH - 1)
@@ -226,23 +239,24 @@
         cf[j].wait_send()
 
 
-REDUCE_SCRATCH = [
-    pltpu.VMEM((64, 2 * HALF), F32), pltpu.VMEM((NCH, 64, CW), F32), pltpu.VMEM((NCH, 64, CW), F32),
-    pltpu.VMEM((NCH, 64, CW), F32), pltpu.VMEM((NCH, 64, CW), F32),
-    pltpu.VMEM((2 * NCH, 1024, CW), BF16), pltpu.SemaphoreType.DMA((6, NCH)), pltpu.SemaphoreType.DMA((2 * NCH,))]
+def reduce_scratch(slots):
+    chunk = pltpu.VMEM((NCH, 64, CW), F32)
+    return [pltpu.VMEM((64, 2 * HALF), F32), chunk, chunk, chunk, chunk, pltpu.VMEM((slots, 1024, CW), BF16),
+            pltpu.SemaphoreType.DMA((6, NCH)), pltpu.SemaphoreType.DMA((slots,))]
+
 
 NAB = 8
 DA = 128
 
 
-def k2_body(o_in, gate_in, h1, onorm, w_out, g2, wattn, clen, alpha, beta,
-            h2_out, qs, kn, vn,
+def k2_body(o_in, gate_in, h1, onorm, w_out, g2, wattn, clen, alpha, beta, vc,
+            h2_out, qs, kn, vn, vpre,
             full, send_a, recv_a, own, recv_x, wo, sems, wosem,
-            xin, ssl, ssr, sssem, abuf, ascr, wd, asem, cosf, sina, sinb):
+            xin, ssl, ssr, sssem, abuf, ascr, wd, asem, cosf, sina, sinb, vsem):
     tp = lax.axis_index('tp')
     nchunk = h1.shape[1] // DA
     wcopies = out_weight_copies(w_out, wo, wosem)
-    for c in wcopies:
+    for c in wcopies[:wo.shape[0]]:
         c.start()
 
     def acopy(i, slot):
@@ -252,7 +266,8 @@
     sq = jnp.zeros((64, 128), F32)
     for h in range(8):
         sq = sq + o_in[h] * o_in[h]
-    ssl[...] = sq
+    wide = jnp.concatenate([sq, jnp.zeros((64, 128), F32)], axis=0).T
+    ssl[...] = jnp.broadcast_to(jnp.sum(wide, axis=0, keepdims=True), (8, 128))
     entry_barrier()
     copies = [pltpu.make_async_remote_copy(src_ref=ssl, dst_ref=ssr.at[k], send_sem=sssem.at[0, k],
                                            recv_sem=sssem.at[1, k], device_id={'tp': dev}, device_id_type=MESH)
@@ -273,7 +288,7 @@
     sinb[...] = jnp.where((lane >= 32) & (lane < 64), sine, 0.0)
     for c in copies:
         c.wait_recv()
-    total = jnp.sum((ssl[...] + ssr[0]) + (ssr[1] + ssr[2]), axis=-1, keepdims=True)
+    total = jnp.broadcast_to(((ssl[...] + ssr[0]) + (ssr[1] + ssr[2]))[0:1], (128, 128)).T[:64]
     inv = lax.rsqrt(total / 4096.0 + EPS)
     for h in range(8):
         xin[:, h * 128:(h + 1) * 128] = (o_in[h] * inv * onorm[h:h + 1] * gate_in[h]).astype(BF16)
@@ -291,12 +306,17 @@
             acopy(i + NAB, slot).start()
         return carry
 
+    vcopy = pltpu.make_async_copy(vc.at[pl.ds(0, NPRE * NB3)], vpre, vsem)
+
     def between(j):
+        if j == 0:
+            vcopy.start()
         lax.fori_loop(j * (nchunk // NCH), (j + 1) * (nchunk // NCH), demix, 0)
 
     reduce_over_tp(xin, wo, wcopies, full, send_a, recv_a, own, recv_x, sems, between)
     for c in copies:
         c.wait_send()
+    vcopy.wait()
     mid = (alpha[0] * h1[...].astype(F32) + beta[0] * full[...]).astype(BF16).astype(F32)
     h2_out[...] = (mid * lax.rsqrt(jnp.mean(mid * mid, axis=-1, keepdims=True) + EPS) * g2[...]).astype(BF16)
     qs[...] = jnp.zeros_like(qs)
@@ -317,29 +337,27 @@
                 vn[kv] = zk.astype(BF16).astype(F32)
 
 
-def k2(o, gate, h1, onorm, w_out, g2, wattn, clen, alpha, beta):
+def k2(o, gate, h1, onorm, w_out, g2, wattn, clen, alpha, beta, vc):
     return pl.pallas_call(
         k2_body,
         out_shape=(jax.ShapeDtypeStruct(h1.shape, BF16), jax.ShapeDtypeStruct((2, 512, 128), F32),
-                   jax.ShapeDtypeStruct((2, 64, 128), F32), jax.ShapeDtypeStruct((2, 64, 128), F32)),
-        in_specs=[VMEM, VMEM, VMEM, VMEM, HBM, VMEM, HBM, SMEM, SMEM, SMEM],
-        out_specs=(VMEM, VMEM, VMEM, VMEM),
-        scratch_shapes=REDUCE_SCRATCH + [
-            pltpu.VMEM((64, 1024), BF16), pltpu.VMEM((64, 128), F32), pltpu.VMEM((3, 64, 128), F32),
+                   jax.ShapeDtypeStruct((2, 64, 128), F32), jax.ShapeDtypeStruct((2, 64, 128), F32),
+                   jax.ShapeDtypeStruct((NPRE * NB3,) + vc.shape[1:], BF16)),
+        in_specs=[VMEM, VMEM, VMEM, VMEM, HBM, VMEM, HBM, SMEM, SMEM, SMEM, HBM],
+        out_specs=(VMEM,) * 5,
+        scratch_shapes=reduce_scratch(4) + [
+            pltpu.VMEM((64, 1024), BF16), pltpu.VMEM((8, 128), F32), pltpu.VMEM((3, 8, 128), F32),
             pltpu.SemaphoreType.DMA((2, 3)),
             pltpu.VMEM((NAB, DA * 12, 128), BF16), pltpu.VMEM((DA * 12, 128), F32),
             pltpu.VMEM((6, 2, h1.shape[1], 128), BF16), pltpu.SemaphoreType.DMA((NAB,)),
-            pltpu.VMEM((64, 128), F32), pltpu.VMEM((64, 128), F32), pltpu.VMEM((64, 128), F32)],
-        compiler_params=pltpu.CompilerParams(vmem_limit_bytes=36 * 2 ** 20, collective_id=0, has_side_effects=True),
+            pltpu.VMEM((64, 128), F32), pltpu.VMEM((64, 128), F32), pltpu.VMEM((64, 128), F32),
+            pltpu.SemaphoreType.DMA],
+        compiler_params=pltpu.CompilerParams(vmem_limit_bytes=29 * 2 ** 20, collective_id=0, has_side_effects=True),
         cost_estimate=pl.CostEstimate(flops=int(6e10), bytes_accessed=int(2e7), transcendentals=0),
-        name='mix_first')(o, gate, h1, onorm, w_out, g2, wattn, clen, alpha, beta)
-
-
-NB3 = 8
-NS3 = 4
-
-
-def k3_body(kc, vc, qs, kn, vn, clen, k_out, v_out, attn, kb, vb, sscr, rsem, wsem):
+        name='mix_first')(o, gate, h1, onorm, w_out, g2, wattn, clen, alpha, beta, vc)
+
+
+def k3_body(kc, vc, vpre, qs, kn, vn, clen, k_out, v_out, attn, kb, vb, sscr, rsem, wsem):
     nstep = kc.shape[0] // NB3
 
     def reads(i, slot):
@@ -349,14 +367,21 @@
         return (pltpu.make_async_copy(kb.at[slot], k_out.at[pl.ds(i * NB3, NB3)], wsem.at[slot, 0]),
                 pltpu.make_async_copy(vb.at[slot], v_out.at[pl.ds(i * NB3, NB3)], wsem.at[slot, 1]))
 
-    for i in range(NS3 - 1):
+    for i in range(NPRE, NS3):
         for c in reads(i, i):
             c.start()
 
     def step(i, carry):
         slot = lax.rem(i, NS3)
-        for c in reads(i, slot):
-            c.wait()
+
+        @pl.when(i < NPRE)
+        def _():
+            vb[slot] = vpre[pl.ds(pl.multiple_of(jnp.minimum(i, NPRE - 1) * NB3, NB3), NB3)]
+
+        @pl.when(i >= NPRE)
+        def _():
+            for c in reads(i, slot):
+                c.wait()
         kb[slot] = kc[pl.ds(i * NB3, NB3)]
         row_id = lax.broadcasted_iota(jnp.int32, (16, 128), 0)
         for u in range(NB3):
@@ -402,14 +427,11 @@
         lax.fori_loop(0, 2, weigh, 0)
         nxt = i + NS3 - 1
 
-        @pl.when(nxt < nstep)
+        @pl.when((i >= 1) & (nxt < nstep))
         def _():
             ps = lax.rem(nxt, NS3)
-
-            @pl.when(i >= 1)
-            def _():
-                for c in writes(i - 1, ps):
-                    c.wait()
+            for c in writes(i - 1, ps):
+                c.wait()
             for c in reads(nxt, ps):
                 c.start()
         return carry
@@ -420,25 +442,25 @@
             c.wait()
 
 
-def k3(kc, vc, qs, kn, vn, clen):
+def k3(kc, vc, vpre, qs, kn, vn, clen):
     shape = (NS3, NB3) + kc.shape[1:]
     return pl.pallas_call(
         k3_body,
         out_shape=(jax.ShapeDtypeStruct(kc.shape, BF16), jax.ShapeDtypeStruct(vc.shape, BF16),
                    jax.ShapeDtypeStruct((512, 128), F32)),
-        in_specs=[VMEM, HBM, VMEM, VMEM, VMEM, SMEM],
+        in_specs=[VMEM, HBM, VMEM, VMEM, VMEM, VMEM, SMEM],
         out_specs=(ANY, ANY, VMEM),
         scratch_shapes=[pltpu.VMEM(shape, BF16), pltpu.VMEM(shape, BF16), pltpu.VMEM((NB3, 8, 512), F32),
                         pltpu.SemaphoreType.DMA((NS3, 2)), pltpu.SemaphoreType.DMA((NS3, 2))],
-        compiler_params=pltpu.CompilerParams(vmem_limit_bytes=20 * 2 ** 20),
+        compiler_params=pltpu.CompilerParams(vmem_limit_bytes=24 * 2 ** 20),
         cost_estimate=pl.CostEstimate(flops=int(1e9), bytes_accessed=int(6e7), transcendentals=0),
-        name='attention')(kc, vc, qs, kn, vn, clen)
+        name='attention')(kc, vc, vpre, qs, kn, vn, clen)
 
 
 def k4_body(attn, h2, w_out, alpha, beta, out,
             full, send_a, recv_a, own, recv_x, wo, sems, wosem, xin):
     wcopies = out_weight_copies(w_out, wo, wosem)
-    for c in wcopies:
+    for c in wcopies[:wo.shape[0]]:
         c.start()
     for r in range(8):
         xin[:, r * 128:(r + 1) * 128] = attn[pl.ds(r, 64, stride=8)].astype(BF16)
@@ -453,7 +475,7 @@
         out_shape=jax.ShapeDtypeStruct(h2.shape, BF16),
         in_specs=[VMEM, VMEM, HBM, SMEM, SMEM],
         out_specs=VMEM,
-        scratch_shapes=REDUCE_SCRATCH + [pltpu.VMEM((64, 1024), BF16)],
+        scratch_shapes=reduce_scratch(2 * NCH) + [pltpu.VMEM((64, 1024), BF16)],
         compiler_params=pltpu.CompilerParams(vmem_limit_bytes=20 * 2 ** 20, collective_id=1, has_side_effects=True),
         cost_estimate=pl.CostEstimate(flops=int(2e10), bytes_accessed=int(2e6), transcendentals=0),
         name='mix_second')(attn, h2, w_out, alpha, beta)
@@ -475,10 +497,11 @@
             return pltpu.with_memory_space_constraint(x, pltpu.HBM)
         state_out, o, gate, h1 = k1(pin(hidden), pin(norm_first.reshape(1, d)), pin(w_qkv.reshape(-1, 128)),
                                     pin(w_gate.reshape(-1, 128)), pin(slopes), pin(lin_state))
+        pinned_v = pin(v_cache)
         wattn = pin(jnp.transpose(w_attn, (0, 2, 1, 3)).reshape(-1, 128))
-        h2, qs, kn, vn = k2(o, gate, h1, out_norm, pin(w_out_lin.reshape(-1, d)), norm_second.reshape(1, d), wattn,
-                            cache_len, mix_alpha, mix_beta)
-        k_out, v_out, attn = k3(k_cache, pin(v_cache), qs, kn, vn, cache_len)
+        h2, qs, kn, vn, vpre = k2(o, gate, h1, out_norm, pin(w_out_lin.reshape(-1, d)), norm_second.reshape(1, d), wattn,
+                            cache_len, mix_alpha, mix_beta, pinned_v)
+        k_out, v_out, attn = k3(k_cache, pinned_v, vpre, qs, kn, vn, cache_len)
         hidden_out = k4(attn, h2, pin(w_out_attn.reshape(-1, d)), mix_alpha, mix_beta)
         return hidden_out, state_out, k_out, v_out
 

time: 108 us -> 104 us (0.963)
  Pallas kernels: 107 us -> 103 us
    pallas_call x1, Pallas kernels: 17.2 us -> 15.5 us  [k3(): pl.pallas_call(k3_body, out_shape=(jax.ShapeDtypeStruct(kc.shape, BF16),...]
    pallas_call x1, Pallas kernels: 39 us -> 37.4 us  [k1(): pl.pallas_call(k1_body, out_shape=(jax.ShapeDtypeStruct(lin.shape, F32),...]
where the time goes in v5:
time: 104 us
  Pallas kernels  103 us (99%)
    pallas_call x1, Pallas kernels, k1(): pl.pallas_call(k1_body, out_shape=(jax.ShapeDtypeStruct(lin.shape, F32),...  37.4 us
    pallas_call x1, Pallas kernels, k2(): pl.pallas_call(k2_body, out_shape=(jax.ShapeDtypeStruct(h1.shape, BF16),...  29.1 us
    pallas_call x1, Pallas kernels, k4(): pl.pallas_call(k4_body, out_shape=jax.ShapeDtypeStruct(h2.shape, BF16), i...  20.7 us
    pallas_call x1, Pallas kernels, k3(): pl.pallas_call(k3_body, out_shape=(jax.ShapeDtypeStruct(kc.shape, BF16),...  15.5 us

profile of v5, /device:TPU:0, one launch (start us, length us, event | category | flops | bytes accessed | tf_op | source)
XLA Modules:
  0.0 104.4 jit_solution(9586313558862352438)
XLA Ops:
  0.6 0.0 copy-start.1
  0.6 0.0 copy-start.2
  0.7 0.0 copy-start.3
  0.7 0.0 copy-start.4
  0.7 0.0 copy-start.5
  0.7 37.4 %lightning.1 = (f32[64,8,128,128]{3,2,1,0:T(8,128)}, f32[8,64,128]{2,1,0:T(8,128)S(1)}, f32[8,64,128]{2,1,0:T(8,128)S(1)}, bf16[64,5120]{1,0:T(8,128)(2,1)S(1)}) custom-call(bf16[64,5120]{1,0:T(8,128)(2,1)} %hid_hbm.1, f32[1,5120]{1,0:T(1,128)} %bitcast.15, bf16[122880,128]{1,0:T(8,128)(2,1)} %bitcast.10, bf16[40960,128]{1,0:T(8,128)(2,1)} %bitcast.12, ...), custom_call_target="tpu_custom_call" | custom-call | flops 999999995904 | bytes 110000000 | tf_op jit(solution)/shard_map/lightning/pallas_call | solution.py:139
  38.1 0.0 copy-done.1
  38.1 0.0 copy-done.2
  38.1 0.0 copy-done.3
  38.1 0.0 copy-done.4
  38.1 0.0 copy-done.5
  38.1 0.0 copy-start
  38.2 29.1 %mix_first.1 = (bf16[64,5120]{1,0:T(8,128)(2,1)S(1)}, f32[2,512,128]{2,1,0:T(8,128)S(1)}, f32[2,64,128]{2,1,0:T(8,128)S(1)}, f32[2,64,128]{2,1,0:T(8,128)S(1)}, bf16[24,2,512,128]{3,2,1,0:T(8,128)(2,1)S(1)}) custom-call(f32[8,64,128]{2,1,0:T(8,128)S(1)} %get-tuple-element.16.o_in, f32[8,64,128]{2,1,0:T(8,128)S(1)} %get-tuple-element.17.gate_in, ...), custom_call_target="tpu_custom_call" | custom-call | flops 60000002048 | bytes 20000000 | tf_op jit(solution)/shard_map/mix_first/pallas_call | solution.py:341
  67.2 0.0 copy-done
  67.3 15.5 %attention.1 = (bf16[64,2,512,128]{3,2,1,0:T(8,128)(2,1)}, bf16[64,2,512,128]{3,2,1,0:T(8,128)(2,1)}, f32[512,128]{1,0:T(8,128)S(1)}) custom-call(bf16[64,2,512,128]{3,2,1,0:T(8,128)(2,1)S(1)} %copy-done, bf16[64,2,512,128]{3,2,1,0:T(8,128)(2,1)} %vc.3, bf16[24,2,512,128]{3,2,1,0:T(8,128)(2,1)S(1)} %get-tuple-element.19.vpre, ...), custom_call_target="tpu_custom_call" | custom-call | flops 1000000000 | bytes 60000000 | tf_op jit(solution)/shard_map/attention/pallas_call | solution.py:447
  82.8 20.7 %mix_second.1 = bf16[64,5120]{1,0:T(8,128)(2,1)S(1)} custom-call(f32[512,128]{1,0:T(8,128)S(1)} %get-tuple-element.23.attn, bf16[64,5120]{1,0:T(8,128)(2,1)S(1)} %get-tuple-element.24.h2, bf16[1024,5120]{1,0:T(8,128)(2,1)} %bitcast.14, f32[2]{0:T(128)S(1)} %copy-done.4, f32[2]{0:T(128)S(1)} %copy-done.5), custom_call_target="tpu_custom_call" | custom-call | flops 20000000000 | bytes 2000000 | tf_op jit(solution)/shard_map/mix_second/pallas_call | solution.py:473
  103.6 0.8 copy.21
Async XLA Ops:
  0.6 37.5 %copy-start.1 = (s32[64]{0:T(128)S(1)}, s32[64]{0:T(128)}, u32[]{:S(2)}) copy-start(s32[64]{0:T(128)} %clen.3) | copy-start | bytes 772
  0.6 37.5 %copy-start.2 = (f32[5120]{0:T(1024)S(1)}, f32[5120]{0:T(1024)}, u32[]{:S(2)}) copy-start(f32[5120]{0:T(1024)} %param.27) | copy-start | bytes 61444
  0.7 37.5 %copy-start.3 = (f32[8,128]{1,0:T(8,128)S(1)}, f32[8,128]{1,0:T(8,128)}, u32[]{:S(2)}) copy-start(f32[8,128]{1,0:T(8,128)} %onorm.1) | copy-start | bytes 12292
  0.7 37.5 %copy-start.4 = (f32[2]{0:T(128)S(1)}, f32[2]{0:T(128)}, u32[]{:S(2)}) copy-start(f32[2]{0:T(128)} %alpha.3) | copy-start | bytes 28
  0.7 37.5 %copy-start.5 = (f32[2]{0:T(128)S(1)}, f32[2]{0:T(128)}, u32[]{:S(2)}) copy-start(f32[2]{0:T(128)} %beta.3) | copy-start | bytes 28
  38.1 29.1 %copy-start = (bf16[64,2,512,128]{3,2,1,0:T(8,128)(2,1)S(1)}, bf16[64,2,512,128]{3,2,1,0:T(8,128)(2,1)}, u32[]{:S(2)}) copy-start(bf16[64,2,512,128]{3,2,1,0:T(8,128)(2,1)} %kc.1) | copy-start | bytes 50331652

commit v6 on v5

--- a/solution.py
+++ b/solution.py
@@ -191,7 +191,7 @@
     return out
 
 
-def reduce_over_tp(xin, wo, wcopies, full, send_a, recv_a, own, recv_x, sems, between):
+def reduce_over_tp(xin, wo, wcopies, full, send_a, recv_a, own, recv_x, sems, between, emit):
     tp = lax.axis_index('tp')
     core = lax.rem(tp, 2)
     partner, across, _ = peers(tp)
@@ -231,8 +231,12 @@
         col = pl.multiple_of(core * HALF + j * CW, CW)
         full[:, pl.ds(col, CW)] = own[j] + recv_x[j]
         cf[j].start()
-    for j in range(NCH):
-        cf[j].wait_recv()
+        emit(col)
+        if j:
+            cf[j - 1].wait_recv()
+            emit(pl.multiple_of((1 - core) * HALF + (j - 1) * CW, CW))
+    cf[NCH - 1].wait_recv()
+    emit(pl.multiple_of((1 - core) * HALF + (NCH - 1) * CW, CW))
     for j in range(NCH):
         ca[j].wait_send()
         cx[j].wait_send()
@@ -313,7 +317,7 @@
             vcopy.start()
         lax.fori_loop(j * (nchunk // NCH), (j + 1) * (nchunk // NCH), demix, 0)
 
-    reduce_over_tp(xin, wo, wcopies, full, send_a, recv_a, own, recv_x, sems, between)
+    reduce_over_tp(xin, wo, wcopies, full, send_a, recv_a, own, recv_x, sems, between, lambda col: None)
     for c in copies:
         c.wait_send()
     vcopy.wait()
@@ -465,8 +469,12 @@
     for r in range(8):
         xin[:, r * 128:(r + 1) * 128] = attn[pl.ds(r, 64, stride=8)].astype(BF16)
     entry_barrier()
-    reduce_over_tp(xin, wo, wcopies, full, send_a, recv_a, own, recv_x, sems, lambda j: None)
-    out[...] = (alpha[1] * h2[...].astype(F32) + beta[1] * full[...]).astype(BF16)
+
+    def emit(col):
+        cols = pl.ds(col, CW)
+        out[:, cols] = (alpha[1] * h2[:, cols].astype(F32) + beta[1] * full[:, cols]).astype(BF16)
+
+    reduce_over_tp(xin, wo, wcopies, full, send_a, recv_a, own, recv_x, sems, lambda j: None, emit)
 
 
 def k4(attn, h2, w_out, alpha, beta):

time: 104 us -> 104 us (level)
  no operation moved by 1% of the time
where the time goes in v6:
time: 104 us
  Pallas kernels  103 us (99%)
    pallas_call x1, Pallas kernels, k1(): pl.pallas_call(k1_body, out_shape=(jax.ShapeDtypeStruct(lin.shape, F32),...  37.4 us
    pallas_call x1, Pallas kernels, k2(): pl.pallas_call(k2_body, out_shape=(jax.ShapeDtypeStruct(h1.shape, BF16),...  29.1 us
    pallas_call x1, Pallas kernels, k4(): pl.pallas_call(k4_body, out_shape=jax.ShapeDtypeStruct(h2.shape, BF16), i...  20.6 us
    pallas_call x1, Pallas kernels, k3(): pl.pallas_call(k3_body, out_shape=(jax.ShapeDtypeStruct(kc.shape, BF16),...  15.5 us

profile of v6, /device:TPU:0, one launch (start us, length us, event | category | flops | bytes accessed | tf_op | source)
XLA Modules:
  0.0 104.2 jit_solution(12770397842509056827)
XLA Ops:
  0.6 0.0 copy-start.1
  0.6 0.0 copy-start.2
  0.7 0.0 copy-start.3
  0.7 0.0 copy-start.4
  0.7 0.0 copy-start.5
  0.7 37.4 %lightning.1 = (f32[64,8,128,128]{3,2,1,0:T(8,128)}, f32[8,64,128]{2,1,0:T(8,128)S(1)}, f32[8,64,128]{2,1,0:T(8,128)S(1)}, bf16[64,5120]{1,0:T(8,128)(2,1)S(1)}) custom-call(bf16[64,5120]{1,0:T(8,128)(2,1)} %hid_hbm.1, f32[1,5120]{1,0:T(1,128)} %bitcast.15, bf16[122880,128]{1,0:T(8,128)(2,1)} %bitcast.10, bf16[40960,128]{1,0:T(8,128)(2,1)} %bitcast.12, ...), custom_call_target="tpu_custom_call" | custom-call | flops 999999995904 | bytes 110000000 | tf_op jit(solution)/shard_map/lightning/pallas_call | solution.py:139
  38.1 0.0 copy-done.1
  38.1 0.0 copy-done.2
  38.1 0.0 copy-done.3
  38.1 0.0 copy-done.4
  38.1 0.0 copy-done.5
  38.1 0.0 copy-start
  38.2 29.1 %mix_first.1 = (bf16[64,5120]{1,0:T(8,128)(2,1)S(1)}, f32[2,512,128]{2,1,0:T(8,128)S(1)}, f32[2,64,128]{2,1,0:T(8,128)S(1)}, f32[2,64,128]{2,1,0:T(8,128)S(1)}, bf16[24,2,512,128]{3,2,1,0:T(8,128)(2,1)S(1)}) custom-call(f32[8,64,128]{2,1,0:T(8,128)S(1)} %get-tuple-element.16.o_in, f32[8,64,128]{2,1,0:T(8,128)S(1)} %get-tuple-element.17.gate_in, ...), custom_call_target="tpu_custom_call" | custom-call | flops 60000002048 | bytes 20000000 | tf_op jit(solution)/shard_map/mix_first/pallas_call | solution.py:345
  67.2 0.0 copy-done
  67.3 15.5 %attention.1 = (bf16[64,2,512,128]{3,2,1,0:T(8,128)(2,1)}, bf16[64,2,512,128]{3,2,1,0:T(8,128)(2,1)}, f32[512,128]{1,0:T(8,128)S(1)}) custom-call(bf16[64,2,512,128]{3,2,1,0:T(8,128)(2,1)S(1)} %copy-done, bf16[64,2,512,128]{3,2,1,0:T(8,128)(2,1)} %vc.3, bf16[24,2,512,128]{3,2,1,0:T(8,128)(2,1)S(1)} %get-tuple-element.19.vpre, ...), custom_call_target="tpu_custom_call" | custom-call | flops 1000000000 | bytes 60000000 | tf_op jit(solution)/shard_map/attention/pallas_call | solution.py:451
  82.8 20.6 %mix_second.1 = bf16[64,5120]{1,0:T(8,128)(2,1)S(1)} custom-call(f32[512,128]{1,0:T(8,128)S(1)} %get-tuple-element.23.attn, bf16[64,5120]{1,0:T(8,128)(2,1)S(1)} %get-tuple-element.24.h2, bf16[1024,5120]{1,0:T(8,128)(2,1)} %bitcast.14, f32[2]{0:T(128)S(1)} %copy-done.4, f32[2]{0:T(128)S(1)} %copy-done.5), custom_call_target="tpu_custom_call" | custom-call | flops 20000000000 | bytes 2000000 | tf_op jit(solution)/shard_map/mix_second/pallas_call | solution.py:481
  103.4 0.8 copy.21
Async XLA Ops:
  0.6 37.5 %copy-start.1 = (s32[64]{0:T(128)S(1)}, s32[64]{0:T(128)}, u32[]{:S(2)}) copy-start(s32[64]{0:T(128)} %clen.3) | copy-start | bytes 772
  0.6 37.5 %copy-start.2 = (f32[5120]{0:T(1024)S(1)}, f32[5120]{0:T(1024)}, u32[]{:S(2)}) copy-start(f32[5120]{0:T(1024)} %param.27) | copy-start | bytes 61444
  0.7 37.5 %copy-start.3 = (f32[8,128]{1,0:T(8,128)S(1)}, f32[8,128]{1,0:T(8,128)}, u32[]{:S(2)}) copy-start(f32[8,128]{1,0:T(8,128)} %onorm.1) | copy-start | bytes 12292
  0.7 37.5 %copy-start.4 = (f32[2]{0:T(128)S(1)}, f32[2]{0:T(128)}, u32[]{:S(2)}) copy-start(f32[2]{0:T(128)} %alpha.3) | copy-start | bytes 28
  0.7 37.5 %copy-start.5 = (f32[2]{0:T(128)S(1)}, f32[2]{0:T(128)}, u32[]{:S(2)}) copy-start(f32[2]{0:T(128)} %beta.3) | copy-start | bytes 28
  38.1 29.1 %copy-start = (bf16[64,2,512,128]{3,2,1,0:T(8,128)(2,1)S(1)}, bf16[64,2,512,128]{3,2,1,0:T(8,128)(2,1)}, u32[]{:S(2)}) copy-start(bf16[64,2,512,128]{3,2,1,0:T(8,128)(2,1)} %kc.1) | copy-start | bytes 50331652

commit v7 on v6

--- a/solution.py
+++ b/solution.py
@@ -317,11 +317,15 @@
             vcopy.start()
         lax.fori_loop(j * (nchunk // NCH), (j + 1) * (nchunk // NCH), demix, 0)
 
-    reduce_over_tp(xin, wo, wcopies, full, send_a, recv_a, own, recv_x, sems, between, lambda col: None)
+    def emit(col):
+        cols = pl.ds(col, CW)
+        h2_out[:, cols] = (alpha[0] * h1[:, cols].astype(F32) + beta[0] * full[:, cols]).astype(BF16)
+
+    reduce_over_tp(xin, wo, wcopies, full, send_a, recv_a, own, recv_x, sems, between, emit)
     for c in copies:
         c.wait_send()
     vcopy.wait()
-    mid = (alpha[0] * h1[...].astype(F32) + beta[0] * full[...]).astype(BF16).astype(F32)
+    mid = h2_out[...].astype(F32)
     h2_out[...] = (mid * lax.rsqrt(jnp.mean(mid * mid, axis=-1, keepdims=True) + EPS) * g2[...]).astype(BF16)
     qs[...] = jnp.zeros_like(qs)
 

time: 104 us -> 104 us (level)
  no operation moved by 1% of the time
where the time goes in v7:
time: 104 us
  Pallas kernels  102 us (98%)
    pallas_call x1, Pallas kernels, k1(): pl.pallas_call(k1_body, out_shape=(jax.ShapeDtypeStruct(lin.shape, F32),...  37.4 us
    pallas_call x1, Pallas kernels, k2(): pl.pallas_call(k2_body, out_shape=(jax.ShapeDtypeStruct(h1.shape, BF16),...  28.9 us
    pallas_call x1, Pallas kernels, k4(): pl.pallas_call(k4_body, out_shape=jax.ShapeDtypeStruct(h2.shape, BF16), i...  20.6 us
    pallas_call x1, Pallas kernels, k3(): pl.pallas_call(k3_body, out_shape=(jax.ShapeDtypeStruct(kc.shape, BF16),...  15.5 us

profile of v7, /device:TPU:0, one launch (start us, length us, event | category | flops | bytes accessed | tf_op | source)
XLA Modules:
  0.0 104.0 jit_solution(3853856425867562979)
XLA Ops:
  0.6 0.0 copy-start.1
  0.6 0.0 copy-start.2
  0.7 0.0 copy-start.3
  0.7 0.0 copy-start.4
  0.7 0.0 copy-start.5
  0.7 37.4 %lightning.1 = (f32[64,8,128,128]{3,2,1,0:T(8,128)}, f32[8,64,128]{2,1,0:T(8,128)S(1)}, f32[8,64,128]{2,1,0:T(8,128)S(1)}, bf16[64,5120]{1,0:T(8,128)(2,1)S(1)}) custom-call(bf16[64,5120]{1,0:T(8,128)(2,1)} %hid_hbm.1, f32[1,5120]{1,0:T(1,128)} %bitcast.15, bf16[122880,128]{1,0:T(8,128)(2,1)} %bitcast.10, bf16[40960,128]{1,0:T(8,128)(2,1)} %bitcast.12, ...), custom_call_target="tpu_custom_call" | custom-call | flops 999999995904 | bytes 110000000 | tf_op jit(solution)/shard_map/lightning/pallas_call | solution.py:139
  38.1 0.0 copy-done.1
  38.1 0.0 copy-done.2
  38.1 0.0 copy-done.3
  38.1 0.0 copy-done.4
  38.1 0.0 copy-done.5
  38.1 0.0 copy-start
  38.2 28.9 %mix_first.1 = (bf16[64,5120]{1,0:T(8,128)(2,1)S(1)}, f32[2,512,128]{2,1,0:T(8,128)S(1)}, f32[2,64,128]{2,1,0:T(8,128)S(1)}, f32[2,64,128]{2,1,0:T(8,128)S(1)}, bf16[24,2,512,128]{3,2,1,0:T(8,128)(2,1)S(1)}) custom-call(f32[8,64,128]{2,1,0:T(8,128)S(1)} %get-tuple-element.16.o_in, f32[8,64,128]{2,1,0:T(8,128)S(1)} %get-tuple-element.17.gate_in, ...), custom_call_target="tpu_custom_call" | custom-call | flops 60000002048 | bytes 20000000 | tf_op jit(solution)/shard_map/mix_first/pallas_call | solution.py:349
  67.0 0.0 copy-done
  67.0 15.5 %attention.1 = (bf16[64,2,512,128]{3,2,1,0:T(8,128)(2,1)}, bf16[64,2,512,128]{3,2,1,0:T(8,128)(2,1)}, f32[512,128]{1,0:T(8,128)S(1)}) custom-call(bf16[64,2,512,128]{3,2,1,0:T(8,128)(2,1)S(1)} %copy-done, bf16[64,2,512,128]{3,2,1,0:T(8,128)(2,1)} %vc.3, bf16[24,2,512,128]{3,2,1,0:T(8,128)(2,1)S(1)} %get-tuple-element.19.vpre, ...), custom_call_target="tpu_custom_call" | custom-call | flops 1000000000 | bytes 60000000 | tf_op jit(solution)/shard_map/attention/pallas_call | solution.py:455
  82.6 20.6 %mix_second.1 = bf16[64,5120]{1,0:T(8,128)(2,1)S(1)} custom-call(f32[512,128]{1,0:T(8,128)S(1)} %get-tuple-element.23.attn, bf16[64,5120]{1,0:T(8,128)(2,1)S(1)} %get-tuple-element.24.h2, bf16[1024,5120]{1,0:T(8,128)(2,1)} %bitcast.14, f32[2]{0:T(128)S(1)} %copy-done.4, f32[2]{0:T(128)S(1)} %copy-done.5), custom_call_target="tpu_custom_call" | custom-call | flops 20000000000 | bytes 2000000 | tf_op jit(solution)/shard_map/mix_second/pallas_call | solution.py:485
  103.1 0.8 copy.21
Async XLA Ops:
  0.6 37.5 %copy-start.1 = (s32[64]{0:T(128)S(1)}, s32[64]{0:T(128)}, u32[]{:S(2)}) copy-start(s32[64]{0:T(128)} %clen.3) | copy-start | bytes 772
  0.6 37.5 %copy-start.2 = (f32[5120]{0:T(1024)S(1)}, f32[5120]{0:T(1024)}, u32[]{:S(2)}) copy-start(f32[5120]{0:T(1024)} %param.27) | copy-start | bytes 61444
  0.7 37.5 %copy-start.3 = (f32[8,128]{1,0:T(8,128)S(1)}, f32[8,128]{1,0:T(8,128)}, u32[]{:S(2)}) copy-start(f32[8,128]{1,0:T(8,128)} %onorm.1) | copy-start | bytes 12292
  0.7 37.5 %copy-start.4 = (f32[2]{0:T(128)S(1)}, f32[2]{0:T(128)}, u32[]{:S(2)}) copy-start(f32[2]{0:T(128)} %alpha.3) | copy-start | bytes 28
  0.7 37.5 %copy-start.5 = (f32[2]{0:T(128)S(1)}, f32[2]{0:T(128)}, u32[]{:S(2)}) copy-start(f32[2]{0:T(128)} %beta.3) | copy-start | bytes 28
  38.1 28.9 %copy-start = (bf16[64,2,512,128]{3,2,1,0:T(8,128)(2,1)S(1)}, bf16[64,2,512,128]{3,2,1,0:T(8,128)(2,1)}, u32[]{:S(2)}) copy-start(bf16[64,2,512,128]{3,2,1,0:T(8,128)(2,1)} %kc.1) | copy-start | bytes 50331652
